TPU v7x, 512 devices: a whole 4x4x16 slice. The times are simulated.
512 devices in a mesh: row: 16 (over z_hi, x, core), col: 32 (over y, z_lo).
Axes of the slice: x: 4, y: 4, z: 16 (z_hi: 2, z_lo: 8; z = z_hi * 8 + z_lo), core: 2. Of those that a mesh axis runs over, the one named last changes fastest.
Arguments:
- geometry: float32 [4, 786432], P(None, ('row', 'col')), may hold values from -1 to 1, as said below
- charges: bfloat16 [32, 786432], P(None, ('row', 'col')), may hold values from -6 to 6
- near_index: int32 [6144, 128], P(('row', 'col')), may hold values from 0 to 4607
- near_count: int32 [6144], P(('row', 'col')), may hold values from 1 to 128
- near_weight: bfloat16 [6144, 128, 128], P(('row', 'col')), may hold values from -0.5 to 0.5
- conductor: int32 [786432], P(('row', 'col')), may hold values from 0 to 31
Outputs:
- potential: float32 [32, 786432], P(None, ('row', 'col'))
- conductor_totals: float32 [32, 32], replicated
Inputs may be any that keep to these rules, and one draw needn't show every extreme that they name: `geometry`: rows 0 to 2 are coordinates in [-1, 1]; row 3 is a panel size in [0.05, 0.2].
All inputs are finite; a program needn't handle non-finite values.
Results may differ from a plain program's by a relative error of at most 0.0044.
Values may be sent and summed in bfloat16 or wider, within the bound.
A program may use at most 64 MiB of HBM per device.

v0:
```python
import jax
import jax.numpy as jnp
from jax import lax
from jax.sharding import PartitionSpec as P

ROUNDS = 8


def passed_along(value, axis, steps):
    count = lax.axis_size(axis)
    pairs = [(source, (source + steps) % count) for source in range(count)]
    return lax.ppermute(value, axis, pairs)


def extended_2(x, sides, width):
    for axis, dim in sides:
        count, length = (lax.axis_size(axis), x.shape[dim])
        up = [(i, (i + 1) % count) for i in range(count)]
        down = [(j, i) for i, j in up]
        last = lax.slice_in_dim(x, length - width, length, axis=dim)
        initial = lax.slice_in_dim(x, 0, width, axis=dim)
        before = lax.ppermute(last, axis, up)
        after = lax.ppermute(initial, axis, down)
        x = jnp.concatenate([before, x, after], axis=dim)
    return x


def kernel_tile(rows, cols):
    delta_x = rows[0][:, None] - cols[0][None, :]
    delta_y = rows[1][:, None] - cols[1][None, :]
    delta_z = rows[2][:, None] - cols[2][None, :]
    spread = rows[3][:, None] * rows[3][:, None] + cols[3][None, :] * cols[3][None, :]
    squared = delta_x * delta_x + delta_y * delta_y + delta_z * delta_z + spread
    return lax.rsqrt(squared).astype(jnp.bfloat16)


def pair_products(own_geo, own_w, other_geo, other_w, backwards):
    panels = own_geo.shape[1]
    rowblk = min(256, panels)
    pieces = []
    back = jnp.zeros(other_w.shape, jnp.float32)
    for start in range(0, panels, rowblk):
        tile = kernel_tile(own_geo[:, start : start + rowblk], other_geo)
        pieces.append(
            lax.dot_general(
                other_w, tile, (((1,), (1,)), ((), ())), preferred_element_type=jnp.float32
            )
        )
        if backwards:
            back = back + jnp.dot(
                own_w[:, start : start + rowblk], tile, preferred_element_type=jnp.float32
            )
    return (jnp.concatenate(pieces, axis=1), back)


def from_lower(geometry, weighted, offset):
    geo = passed_along(geometry, ("row", "col"), offset)
    wts = passed_along(weighted, ("row", "col"), offset)
    return (geo, wts)


def give_back(partial_value, offset):
    return passed_along(partial_value, ("row", "col"), -offset)


def on_device(geometry, charges, near_index, near_count, near_weight, conductor):
    devices = lax.axis_size(("row", "col"))
    stride = devices // (2 * ROUNDS)
    offsets = [1 + k * stride for k in range(ROUNDS)]
    panels = charges.shape[1]
    groups_dev = near_index.shape[0]
    area = geometry[3] * geometry[3]
    weighted = (charges.astype(jnp.float32) * area[None, :]).astype(jnp.bfloat16)
    field, unused = pair_products(geometry, weighted, geometry, weighted, False)
    for turn in range(ROUNDS):
        offset = offsets[turn]
        lower_geo, lower_w = from_lower(geometry, weighted, offset)
        forward, back = pair_products(geometry, weighted, lower_geo, lower_w, True)
        field = field + forward + give_back(back.astype(jnp.bfloat16), offset).astype(jnp.float32)
    extended = extended_2(charges, ((("row", "col"), 1),), panels)
    gathered = jnp.take(extended, near_index.reshape(-1), axis=1).reshape(
        charges.shape[0], groups_dev, near_index.shape[1]
    )
    live = jnp.arange(near_index.shape[1], dtype=jnp.int32)[None, :] < near_count[:, None]
    gathered = jnp.where(live[None], gathered, jnp.zeros_like(gathered))
    correction = jnp.einsum(
        "rgk,gtk->rgt", gathered, near_weight, preferred_element_type=jnp.float32
    )
    field = field + correction.reshape(charges.shape[0], panels)
    member = (conductor[:, None] == jnp.arange(charges.shape[0], dtype=jnp.int32)[None, :]).astype(
        jnp.float32
    )
    local_totals = jnp.dot(
        field * area[None, :],
        member,
        precision=lax.Precision.HIGHEST,
        preferred_element_type=jnp.float32,
    )
    totals = lax.psum(local_totals, ("row", "col"))
    return (field, totals)


def solution(mesh):
    in_specs = (
        P(None, ("row", "col")),
        P(None, ("row", "col")),
        P(("row", "col"), None),
        P(("row", "col")),
        P(("row", "col"), None, None),
        P(("row", "col")),
    )
    out_specs = (P(None, ("row", "col")), P())
    return jax.shard_map(
        on_device, mesh=mesh, in_specs=in_specs, out_specs=out_specs, check_vma=False
    )
```

profile of v0, /device:TPU:1, one launch (start us, length us, event | category | flops | bytes accessed | tf_op | source)
XLA Modules:
  0.0 440.3 jit_solution(11019835576902463426)
XLA Ops:
  0.6 16.8 %collective-permute-start.25 = (bf16[32,1536]{1,0:T(8,128)(2,1)}, bf16[32,1536]{1,0:T(8,128)(2,1)}, u32[]{:S(2)}, u32[]{:S(2)}) collective-permute-start(bf16[32,1536]{1,0:T(8,128)(2,1)} %param.7), channel_id=1, source_target_pairs={{1,0},{2,1},{3,2},{4,3},{5,4},{6,5},{7,6},{8,7},{9,8},{10,9},{11,1... | collective-permute-start | bytes 294920 | tf_op jit(solution)/shard_map/ppermute | solution.py:23
  17.5 1.9 collective-permute-start.24
  19.4 3.6 collective-permute-start.22
  23.0 4.8 %collective-permute-start.19 = (f32[4,1536]{1,0:T(4,128)}, f32[4,1536]{1,0:T(4,128)S(1)}, u32[]{:S(2)}, u32[]{:S(2)}) collective-permute-start(f32[4,1536]{1,0:T(4,128)} %param.6), channel_id=1, source_target_pairs={{0,193},{1,194},{2,195},{3,196},{4,197},{5,198},{6,199},{7,200},{8... | collective-permute-start | bytes 73736 | tf_op jit(solution)/shard_map/ppermute | solution.py:12
  27.9 0.9 slice_reduce_fusion.26
  28.8 0.9 multiply_convert_fusion
  29.7 2.2 collective-permute-start.21
  31.9 0.8 fusion.128
  32.8 0.9 fusion.127
  34.4 1.4 iota_compare_fusion.2
  35.8 1.8 convolution_dynamic-update-slice_fusion.53
  37.6 0.8 convolution_dynamic-update-slice_fusion.52
  38.4 0.8 convolution_dynamic-update-slice_fusion.51
  39.2 0.8 convolution_dynamic-update-slice_fusion.50
  40.0 0.8 convolution_dynamic-update-slice_fusion.49
  40.8 0.8 convolution_dynamic-update-slice_fusion.48
  41.6 9.9 %collective-permute-start.18 = (bf16[32,1536]{1,0:T(8,128)(2,1)S(1)}, bf16[32,1536]{1,0:T(8,128)(2,1)S(1)}, u32[]{:S(2)}, u32[]{:S(2)}) collective-permute-start(bf16[32,1536]{1,0:T(8,128)(2,1)S(1)} %multiply_convert_fusion), channel_id=1, source_target_pairs={{0,193},{1,194},{2,195},{3,196},{4,197},{5,198},{6,199},{7,200},{8... | collective-permute-start | bytes 294920 | tf_op jit(solution)/shard_map/ppermute | solution.py:12
  52.3 0.8 convolution_add_fusion.4
  55.6 1.4 fusion.7
  57.0 4.6 %collective-permute-start.16 = (f32[4,1536]{1,0:T(4,128)S(1)}, f32[4,1536]{1,0:T(4,128)S(1)}, u32[]{:S(2)}, u32[]{:S(2)}) collective-permute-start(f32[4,1536]{1,0:T(4,128)S(1)} %copy-done.5), channel_id=1, source_target_pairs={{0,161},{1,162},{2,163},{3,164},{4,165},{5,166},{6,167},{7,168},{8... | collective-permute-start | bytes 73736 | tf_op jit(solution)/shard_map/ppermute | solution.py:12
  62.5 0.8 convolution_add_fusion.9
  65.7 1.4 fusion.6
  67.1 7.2 %collective-permute-start.13 = (f32[4,1536]{1,0:T(4,128)S(1)}, f32[4,1536]{1,0:T(4,128)S(1)}, u32[]{:S(2)}, u32[]{:S(2)}) collective-permute-start(f32[4,1536]{1,0:T(4,128)S(1)} %copy-done.5), channel_id=1, source_target_pairs={{0,129},{1,130},{2,131},{3,132},{4,133},{5,134},{6,135},{7,136},{8... | collective-permute-start | bytes 73736 | tf_op jit(solution)/shard_map/ppermute | solution.py:12
  75.2 0.8 convolution_add_fusion.14
  78.4 1.4 fusion.5
  79.8 11.6 %collective-permute-start.10 = (f32[4,1536]{1,0:T(4,128)S(1)}, f32[4,1536]{1,0:T(4,128)S(1)}, u32[]{:S(2)}, u32[]{:S(2)}) collective-permute-start(f32[4,1536]{1,0:T(4,128)S(1)} %copy-done.5), channel_id=1, source_target_pairs={{0,97},{1,98},{2,99},{3,100},{4,101},{5,102},{6,103},{7,104},{8,10... | collective-permute-start | bytes 73736 | tf_op jit(solution)/shard_map/ppermute | solution.py:12
  92.3 0.8 convolution_add_fusion.19
  95.5 1.4 fusion.4
  97.0 9.3 %collective-permute-start.7 = (f32[4,1536]{1,0:T(4,128)S(1)}, f32[4,1536]{1,0:T(4,128)S(1)}, u32[]{:S(2)}, u32[]{:S(2)}) collective-permute-start(f32[4,1536]{1,0:T(4,128)S(1)} %copy-done.5), channel_id=1, source_target_pairs={{0,65},{1,66},{2,67},{3,68},{4,69},{5,70},{6,71},{7,72},{8,73},{9,... | collective-permute-start | bytes 73736 | tf_op jit(solution)/shard_map/ppermute | solution.py:12
  107.1 0.8 convolution_add_fusion.24
  107.9 0.8 convolution_add_fusion.23
  108.7 0.8 convolution_add_fusion.22
  109.5 0.8 convolution_add_fusion.21
  110.3 1.4 fusion.3
  111.8 6.9 %collective-permute-start.4 = (f32[4,1536]{1,0:T(4,128)S(1)}, f32[4,1536]{1,0:T(4,128)S(1)}, u32[]{:S(2)}, u32[]{:S(2)}) collective-permute-start(f32[4,1536]{1,0:T(4,128)S(1)} %copy-done.5), channel_id=1, source_target_pairs={{0,33},{1,34},{2,35},{3,36},{4,37},{5,38},{6,39},{7,40},{8,41},{9,... | collective-permute-start | bytes 73736 | tf_op jit(solution)/shard_map/ppermute | solution.py:12
  119.5 0.8 convolution_add_fusion.29
  122.7 1.4 fusion.2
  124.2 7.0 %collective-permute-start.1 = (f32[4,1536]{1,0:T(4,128)S(1)}, f32[4,1536]{1,0:T(4,128)S(1)}, u32[]{:S(2)}, u32[]{:S(2)}) collective-permute-start(f32[4,1536]{1,0:T(4,128)S(1)} %copy-done.5), channel_id=1, source_target_pairs={{0,1},{1,2},{2,3},{3,4},{4,5},{5,6},{6,7},{7,8},{8,9},{9,10},{10,1... | collective-permute-start | bytes 73736 | tf_op jit(solution)/shard_map/ppermute | solution.py:12
  132.0 0.8 convolution_add_fusion.34
  135.2 1.4 fusion.1
  136.6 14.7 %collective-permute-done.1 = f32[4,1536]{1,0:T(4,128)S(1)} collective-permute-done((f32[4,1536]{1,0:T(4,128)S(1)}, f32[4,1536]{1,0:T(4,128)S(1)}, u32[]{:S(2)}, u32[]{:S(2)}) %collective-permute-start.1) | collective-permute-done | bytes 24608 | tf_op jit(solution)/shard_map/ppermute | solution.py:12
  151.3 2.4 collective-permute-start.15
  154.5 0.8 convolution_add_fusion.39
  155.4 0.8 convolution_add_fusion.38
  157.8 1.4 fusion
  159.2 1.9 collective-permute-start.12
  165.9 8.6 %collective-permute-start.9 = (bf16[32,1536]{1,0:T(8,128)(2,1)S(1)}, bf16[32,1536]{1,0:T(8,128)(2,1)S(1)}, u32[]{:S(2)}, u32[]{:S(2)}) collective-permute-start(bf16[32,1536]{1,0:T(8,128)(2,1)S(1)} %multiply_convert_fusion), channel_id=1, source_target_pairs={{0,97},{1,98},{2,99},{3,100},{4,101},{5,102},{6,103},{7,104},{8,10... | collective-permute-start | bytes 294920 | tf_op jit(solution)/shard_map/ppermute | solution.py:12
  179.2 38.7 %collective-permute-start.6 = (bf16[32,1536]{1,0:T(8,128)(2,1)S(1)}, bf16[32,1536]{1,0:T(8,128)(2,1)S(1)}, u32[]{:S(2)}, u32[]{:S(2)}) collective-permute-start(bf16[32,1536]{1,0:T(8,128)(2,1)S(1)} %multiply_convert_fusion), channel_id=1, source_target_pairs={{0,65},{1,66},{2,67},{3,68},{4,69},{5,70},{6,71},{7,72},{8,73},{9,... | collective-permute-start | bytes 294920 | tf_op jit(solution)/shard_map/ppermute | solution.py:12
  222.7 2.1 collective-permute-start.3
  229.6 1.9 collective-permute-start
  236.2 5.3 %collective-permute-start.23 = (bf16[32,1536]{1,0:T(8,128)(2,1)}, bf16[32,1536]{1,0:T(8,128)(2,1)}, u32[]{:S(2)}, u32[]{:S(2)}) collective-permute-start(bf16[32,1536]{1,0:T(8,128)(2,1)} %fusion.7), channel_id=1, source_target_pairs={{0,287},{1,288},{2,289},{3,290},{4,291},{5,292},{6,293},{7,294},{8... | collective-permute-start | bytes 294920 | tf_op jit(solution)/shard_map/ppermute | solution.py:12
  246.3 1.9 collective-permute-start.20
  253.0 1.9 collective-permute-start.17
  258.8 1.9 collective-permute-start.14
  260.8 7.1 %collective-permute-start.11 = (bf16[32,1536]{1,0:T(8,128)(2,1)}, bf16[32,1536]{1,0:T(8,128)(2,1)}, u32[]{:S(2)}, u32[]{:S(2)}) collective-permute-start(bf16[32,1536]{1,0:T(8,128)(2,1)} %fusion.3), channel_id=1, source_target_pairs={{0,415},{1,416},{2,417},{3,418},{4,419},{5,420},{6,421},{7,422},{8... | collective-permute-start | bytes 294920 | tf_op jit(solution)/shard_map/ppermute | solution.py:12
  267.9 1.0 pad_maximum_fusion
  270.2 3.2 gather_fusion
  273.6 1.9 collective-permute-start.8
  275.5 3.3 collective-permute-start.5
  278.9 44.2 %collective-permute-start.2 = (bf16[32,1536]{1,0:T(8,128)(2,1)}, bf16[32,1536]{1,0:T(8,128)(2,1)S(1)}, u32[]{:S(2)}, u32[]{:S(2)}) collective-permute-start(bf16[32,1536]{1,0:T(8,128)(2,1)} %fusion), channel_id=1, source_target_pairs={{0,511},{1,0},{2,1},{3,2},{4,3},{5,4},{6,5},{7,6},{8,7},{9,8},{10,... | collective-permute-start | bytes 294920 | tf_op jit(solution)/shard_map/ppermute | solution.py:12
  323.0 1.0 convolution_bitcast_fusion
  324.1 0.9 collective-permute-done.2
  325.0 1.3 bitcast_add_fusion
  326.7 113.1 %psum.7 = f32[32,32]{1,0:T(8,128)} all-reduce(f32[32,32]{1,0:T(8,128)S(1)} %fusion.50), channel_id=1, replica_groups=mesh['row'=16,'col'=32] {'row','col'}, use_global_device_ids=true, to_apply=%region_0.1 | all-reduce | flops 1024 | bytes 8192 | tf_op jit(solution)/shard_map/psum | solution.py:99
  (127 shorter events, 62.2 us)
Async XLA Ops:
  0.6 322.4 %copy-start = (bf16[12,128,128]{2,1,0:T(8,128)(2,1)S(1)}, bf16[12,128,128]{2,1,0:T(8,128)(2,1)}, u32[]{:S(2)}) copy-start(bf16[12,128,128]{2,1,0:T(8,128)(2,1)} %param.10) | copy-start | bytes 1179652
  0.6 258.2 %collective-permute-start.25 = (bf16[32,1536]{1,0:T(8,128)(2,1)}, bf16[32,1536]{1,0:T(8,128)(2,1)}, u32[]{:S(2)}, u32[]{:S(2)}) collective-permute-start(bf16[32,1536]{1,0:T(8,128)(2,1)} %param.7), channel_id=1, source_target_pairs={{1,0},{2,1},{3,2},{4,3},{5,4},{6,5},{7,6},{8,7},{9,8},{10,9},{11,1... | collective-permute-start | bytes 294920 | tf_op jit(solution)/shard_map/ppermute | solution.py:23
  17.5 243.3 %collective-permute-start.24 = (bf16[32,1536]{1,0:T(8,128)(2,1)}, bf16[32,1536]{1,0:T(8,128)(2,1)}, u32[]{:S(2)}, u32[]{:S(2)}) collective-permute-start(bf16[32,1536]{1,0:T(8,128)(2,1)} %param.7), channel_id=1, source_target_pairs={{0,1},{1,2},{2,3},{3,4},{4,5},{5,6},{6,7},{7,8},{8,9},{9,10},{10,1... | collective-permute-start | bytes 294920 | tf_op jit(solution)/shard_map/ppermute | solution.py:22
  19.4 22.2 %collective-permute-start.22 = (f32[4,1536]{1,0:T(4,128)}, f32[4,1536]{1,0:T(4,128)S(1)}, u32[]{:S(2)}, u32[]{:S(2)}) collective-permute-start(f32[4,1536]{1,0:T(4,128)} %param.6), channel_id=1, source_target_pairs={{0,225},{1,226},{2,227},{3,228},{4,229},{5,230},{6,231},{7,232},{8... | collective-permute-start | bytes 73736 | tf_op jit(solution)/shard_map/ppermute | solution.py:12
  23.0 34.0 %collective-permute-start.19 = (f32[4,1536]{1,0:T(4,128)}, f32[4,1536]{1,0:T(4,128)S(1)}, u32[]{:S(2)}, u32[]{:S(2)}) collective-permute-start(f32[4,1536]{1,0:T(4,128)} %param.6), channel_id=1, source_target_pairs={{0,193},{1,194},{2,195},{3,196},{4,197},{5,198},{6,199},{7,200},{8... | collective-permute-start | bytes 73736 | tf_op jit(solution)/shard_map/ppermute | solution.py:12
  29.7 129.5 %collective-permute-start.21 = (bf16[32,1536]{1,0:T(8,128)(2,1)S(1)}, bf16[32,1536]{1,0:T(8,128)(2,1)S(1)}, u32[]{:S(2)}, u32[]{:S(2)}) collective-permute-start(bf16[32,1536]{1,0:T(8,128)(2,1)S(1)} %multiply_convert_fusion), channel_id=1, source_target_pairs={{0,225},{1,226},{2,227},{3,228},{4,229},{5,230},{6,231},{7,232},{8... | collective-permute-start | bytes 294920 | tf_op jit(solution)/shard_map/ppermute | solution.py:12
  35.8 1.8 copy-start.1
  41.6 124.2 %collective-permute-start.18 = (bf16[32,1536]{1,0:T(8,128)(2,1)S(1)}, bf16[32,1536]{1,0:T(8,128)(2,1)S(1)}, u32[]{:S(2)}, u32[]{:S(2)}) collective-permute-start(bf16[32,1536]{1,0:T(8,128)(2,1)S(1)} %multiply_convert_fusion), channel_id=1, source_target_pairs={{0,193},{1,194},{2,195},{3,196},{4,197},{5,198},{6,199},{7,200},{8... | collective-permute-start | bytes 294920 | tf_op jit(solution)/shard_map/ppermute | solution.py:12
  55.5 1.5 copy-start.5
  57.0 10.1 %collective-permute-start.16 = (f32[4,1536]{1,0:T(4,128)S(1)}, f32[4,1536]{1,0:T(4,128)S(1)}, u32[]{:S(2)}, u32[]{:S(2)}) collective-permute-start(f32[4,1536]{1,0:T(4,128)S(1)} %copy-done.5), channel_id=1, source_target_pairs={{0,161},{1,162},{2,163},{3,164},{4,165},{5,166},{6,167},{7,168},{8... | collective-permute-start | bytes 73736 | tf_op jit(solution)/shard_map/ppermute | solution.py:12
  67.1 12.7 %collective-permute-start.13 = (f32[4,1536]{1,0:T(4,128)S(1)}, f32[4,1536]{1,0:T(4,128)S(1)}, u32[]{:S(2)}, u32[]{:S(2)}) collective-permute-start(f32[4,1536]{1,0:T(4,128)S(1)} %copy-done.5), channel_id=1, source_target_pairs={{0,129},{1,130},{2,131},{3,132},{4,133},{5,134},{6,135},{7,136},{8... | collective-permute-start | bytes 73736 | tf_op jit(solution)/shard_map/ppermute | solution.py:12
  79.8 17.1 %collective-permute-start.10 = (f32[4,1536]{1,0:T(4,128)S(1)}, f32[4,1536]{1,0:T(4,128)S(1)}, u32[]{:S(2)}, u32[]{:S(2)}) collective-permute-start(f32[4,1536]{1,0:T(4,128)S(1)} %copy-done.5), channel_id=1, source_target_pairs={{0,97},{1,98},{2,99},{3,100},{4,101},{5,102},{6,103},{7,104},{8,10... | collective-permute-start | bytes 73736 | tf_op jit(solution)/shard_map/ppermute | solution.py:12
  97.0 14.8 %collective-permute-start.7 = (f32[4,1536]{1,0:T(4,128)S(1)}, f32[4,1536]{1,0:T(4,128)S(1)}, u32[]{:S(2)}, u32[]{:S(2)}) collective-permute-start(f32[4,1536]{1,0:T(4,128)S(1)} %copy-done.5), channel_id=1, source_target_pairs={{0,65},{1,66},{2,67},{3,68},{4,69},{5,70},{6,71},{7,72},{8,73},{9,... | collective-permute-start | bytes 73736 | tf_op jit(solution)/shard_map/ppermute | solution.py:12
  111.8 12.4 %collective-permute-start.4 = (f32[4,1536]{1,0:T(4,128)S(1)}, f32[4,1536]{1,0:T(4,128)S(1)}, u32[]{:S(2)}, u32[]{:S(2)}) collective-permute-start(f32[4,1536]{1,0:T(4,128)S(1)} %copy-done.5), channel_id=1, source_target_pairs={{0,33},{1,34},{2,35},{3,36},{4,37},{5,38},{6,39},{7,40},{8,41},{9,... | collective-permute-start | bytes 73736 | tf_op jit(solution)/shard_map/ppermute | solution.py:12
  124.2 27.1 %collective-permute-start.1 = (f32[4,1536]{1,0:T(4,128)S(1)}, f32[4,1536]{1,0:T(4,128)S(1)}, u32[]{:S(2)}, u32[]{:S(2)}) collective-permute-start(f32[4,1536]{1,0:T(4,128)S(1)} %copy-done.5), channel_id=1, source_target_pairs={{0,1},{1,2},{2,3},{3,4},{4,5},{5,6},{6,7},{7,8},{8,9},{9,10},{10,1... | collective-permute-start | bytes 73736 | tf_op jit(solution)/shard_map/ppermute | solution.py:12
  151.3 27.9 %collective-permute-start.15 = (bf16[32,1536]{1,0:T(8,128)(2,1)S(1)}, bf16[32,1536]{1,0:T(8,128)(2,1)S(1)}, u32[]{:S(2)}, u32[]{:S(2)}) collective-permute-start(bf16[32,1536]{1,0:T(8,128)(2,1)S(1)} %multiply_convert_fusion), channel_id=1, source_target_pairs={{0,161},{1,162},{2,163},{3,164},{4,165},{5,166},{6,167},{7,168},{8... | collective-permute-start | bytes 294920 | tf_op jit(solution)/shard_map/ppermute | solution.py:12
  159.2 63.5 %collective-permute-start.12 = (bf16[32,1536]{1,0:T(8,128)(2,1)S(1)}, bf16[32,1536]{1,0:T(8,128)(2,1)S(1)}, u32[]{:S(2)}, u32[]{:S(2)}) collective-permute-start(bf16[32,1536]{1,0:T(8,128)(2,1)S(1)} %multiply_convert_fusion), channel_id=1, source_target_pairs={{0,129},{1,130},{2,131},{3,132},{4,133},{5,134},{6,135},{7,136},{8... | collective-permute-start | bytes 294920 | tf_op jit(solution)/shard_map/ppermute | solution.py:12
  165.9 63.7 %collective-permute-start.9 = (bf16[32,1536]{1,0:T(8,128)(2,1)S(1)}, bf16[32,1536]{1,0:T(8,128)(2,1)S(1)}, u32[]{:S(2)}, u32[]{:S(2)}) collective-permute-start(bf16[32,1536]{1,0:T(8,128)(2,1)S(1)} %multiply_convert_fusion), channel_id=1, source_target_pairs={{0,97},{1,98},{2,99},{3,100},{4,101},{5,102},{6,103},{7,104},{8,10... | collective-permute-start | bytes 294920 | tf_op jit(solution)/shard_map/ppermute | solution.py:12
  179.2 57.0 %collective-permute-start.6 = (bf16[32,1536]{1,0:T(8,128)(2,1)S(1)}, bf16[32,1536]{1,0:T(8,128)(2,1)S(1)}, u32[]{:S(2)}, u32[]{:S(2)}) collective-permute-start(bf16[32,1536]{1,0:T(8,128)(2,1)S(1)} %multiply_convert_fusion), channel_id=1, source_target_pairs={{0,65},{1,66},{2,67},{3,68},{4,69},{5,70},{6,71},{7,72},{8,73},{9,... | collective-permute-start | bytes 294920 | tf_op jit(solution)/shard_map/ppermute | solution.py:12
  222.7 23.6 %collective-permute-start.3 = (bf16[32,1536]{1,0:T(8,128)(2,1)S(1)}, bf16[32,1536]{1,0:T(8,128)(2,1)S(1)}, u32[]{:S(2)}, u32[]{:S(2)}) collective-permute-start(bf16[32,1536]{1,0:T(8,128)(2,1)S(1)} %multiply_convert_fusion), channel_id=1, source_target_pairs={{0,33},{1,34},{2,35},{3,36},{4,37},{5,38},{6,39},{7,40},{8,41},{9,... | collective-permute-start | bytes 294920 | tf_op jit(solution)/shard_map/ppermute | solution.py:12
  229.6 23.4 %collective-permute-start = (bf16[32,1536]{1,0:T(8,128)(2,1)S(1)}, bf16[32,1536]{1,0:T(8,128)(2,1)S(1)}, u32[]{:S(2)}, u32[]{:S(2)}) collective-permute-start(bf16[32,1536]{1,0:T(8,128)(2,1)S(1)} %multiply_convert_fusion), channel_id=1, source_target_pairs={{0,1},{1,2},{2,3},{3,4},{4,5},{5,6},{6,7},{7,8},{8,9},{9,10},{10,1... | collective-permute-start | bytes 294920 | tf_op jit(solution)/shard_map/ppermute | solution.py:12
  236.2 37.3 %collective-permute-start.23 = (bf16[32,1536]{1,0:T(8,128)(2,1)}, bf16[32,1536]{1,0:T(8,128)(2,1)}, u32[]{:S(2)}, u32[]{:S(2)}) collective-permute-start(bf16[32,1536]{1,0:T(8,128)(2,1)} %fusion.7), channel_id=1, source_target_pairs={{0,287},{1,288},{2,289},{3,290},{4,291},{5,292},{6,293},{7,294},{8... | collective-permute-start | bytes 294920 | tf_op jit(solution)/shard_map/ppermute | solution.py:12
  246.3 29.2 %collective-permute-start.20 = (bf16[32,1536]{1,0:T(8,128)(2,1)}, bf16[32,1536]{1,0:T(8,128)(2,1)}, u32[]{:S(2)}, u32[]{:S(2)}) collective-permute-start(bf16[32,1536]{1,0:T(8,128)(2,1)} %fusion.6), channel_id=1, source_target_pairs={{0,319},{1,320},{2,321},{3,322},{4,323},{5,324},{6,325},{7,326},{8... | collective-permute-start | bytes 294920 | tf_op jit(solution)/shard_map/ppermute | solution.py:12
  252.9 2.7 copy-start.3
  253.0 25.9 %collective-permute-start.17 = (bf16[32,1536]{1,0:T(8,128)(2,1)}, bf16[32,1536]{1,0:T(8,128)(2,1)}, u32[]{:S(2)}, u32[]{:S(2)}) collective-permute-start(bf16[32,1536]{1,0:T(8,128)(2,1)} %fusion.5), channel_id=1, source_target_pairs={{0,351},{1,352},{2,353},{3,354},{4,355},{5,356},{6,357},{7,358},{8... | collective-permute-start | bytes 294920 | tf_op jit(solution)/shard_map/ppermute | solution.py:12
  258.8 65.2 %collective-permute-start.14 = (bf16[32,1536]{1,0:T(8,128)(2,1)}, bf16[32,1536]{1,0:T(8,128)(2,1)}, u32[]{:S(2)}, u32[]{:S(2)}) collective-permute-start(bf16[32,1536]{1,0:T(8,128)(2,1)} %fusion.4), channel_id=1, source_target_pairs={{0,383},{1,384},{2,385},{3,386},{4,387},{5,388},{6,389},{7,390},{8... | collective-permute-start | bytes 294920 | tf_op jit(solution)/shard_map/ppermute | solution.py:12
  260.8 63.3 %collective-permute-start.11 = (bf16[32,1536]{1,0:T(8,128)(2,1)}, bf16[32,1536]{1,0:T(8,128)(2,1)}, u32[]{:S(2)}, u32[]{:S(2)}) collective-permute-start(bf16[32,1536]{1,0:T(8,128)(2,1)} %fusion.3), channel_id=1, source_target_pairs={{0,415},{1,416},{2,417},{3,418},{4,419},{5,420},{6,421},{7,422},{8... | collective-permute-start | bytes 294920 | tf_op jit(solution)/shard_map/ppermute | solution.py:12
  273.4 51.6 %copy-start.4 = (f32[32,1536]{1,0:T(8,128)S(1)}, f32[32,1536]{1,0:T(8,128)}, u32[]{:S(2)}) copy-start(f32[32,1536]{1,0:T(8,128)} %copy-done.3) | copy-start | bytes 589828
  273.6 50.5 %collective-permute-start.8 = (bf16[32,1536]{1,0:T(8,128)(2,1)}, bf16[32,1536]{1,0:T(8,128)(2,1)S(1)}, u32[]{:S(2)}, u32[]{:S(2)}) collective-permute-start(bf16[32,1536]{1,0:T(8,128)(2,1)} %fusion.2), channel_id=1, source_target_pairs={{0,447},{1,448},{2,449},{3,450},{4,451},{5,452},{6,453},{7,454},{8... | collective-permute-start | bytes 294920 | tf_op jit(solution)/shard_map/ppermute | solution.py:12
  275.5 48.5 %collective-permute-start.5 = (bf16[32,1536]{1,0:T(8,128)(2,1)}, bf16[32,1536]{1,0:T(8,128)(2,1)S(1)}, u32[]{:S(2)}, u32[]{:S(2)}) collective-permute-start(bf16[32,1536]{1,0:T(8,128)(2,1)} %fusion.1), channel_id=1, source_target_pairs={{0,479},{1,480},{2,481},{3,482},{4,483},{5,484},{6,485},{7,486},{8... | collective-permute-start | bytes 294920 | tf_op jit(solution)/shard_map/ppermute | solution.py:12
  278.9 46.1 %collective-permute-start.2 = (bf16[32,1536]{1,0:T(8,128)(2,1)}, bf16[32,1536]{1,0:T(8,128)(2,1)S(1)}, u32[]{:S(2)}, u32[]{:S(2)}) collective-permute-start(bf16[32,1536]{1,0:T(8,128)(2,1)} %fusion), channel_id=1, source_target_pairs={{0,511},{1,0},{2,1},{3,2},{4,3},{5,4},{6,5},{7,6},{8,7},{9,8},{10,... | collective-permute-start | bytes 294920 | tf_op jit(solution)/shard_map/ppermute | solution.py:12
  324.0 2.2 copy-start.6
  326.2 113.6 %copy-start.2 = (f32[32,1536]{1,0:T(8,128)}, f32[32,1536]{1,0:T(8,128)S(1)}, u32[]{:S(2)}) copy-start(f32[32,1536]{1,0:T(8,128)S(1)} %bitcast_add_fusion) | copy-start | bytes 589828
where the time goes:
time: 449 us; the launch traced here: 440 us
  starting transfers between devices  209 us (47%)
  blocking collectives  113 us (25%)
  matrix products  87.9 us (20%)
  waiting for transfers between devices  15.6 us (3%)
  other arithmetic  8.44 us (2%)
    ppermute x24, starting transfers between devices, passed_along(): return lax.ppermute(value, axis, pairs)  190 us
    psum x1, blocking collectives, on_device(): totals = lax.psum(local_totals, ('row', 'col'))  113 us
    dot_general x48, matrix products, pair_products(): jnp.dot(own_w[:, start:start + rowblk], tile, preferred_element_type=jnp....  43.2 us
    dot_general x54, matrix products, pair_products(): lax.dot_general(other_w, tile, (((1,), (1,)), ((), ())), preferred_elemen...  43.2 us
    ppermute x1, starting transfers between devices, extended_2(): after = lax.ppermute(initial, axis, down)  16.8 us
    ppermute x24, waiting for transfers between devices, passed_along(): return lax.ppermute(value, axis, pairs)  15.6 us
  transfers between devices with their start and end apart: 26, of which 2 were waited for; matrix products, arithmetic and copies ran while one was open for 22% of the time, Pallas kernels for 0%

commit v1 on v0

v1 whole, which is shorter than its diff:
```python
import functools

import jax
import jax.numpy as jnp
from jax import lax
from jax.experimental import pallas as pl
from jax.experimental.pallas import tpu as pltpu
from jax.sharding import PartitionSpec as P

MESH = pl.DeviceIdType.MESH
BLOCK = 1536
RHS = 32
GROUPS = 12
ROWBLK = 256
ROWS = 16
COLS = 32
F32 = jnp.float32
BF16 = jnp.bfloat16
VMEM = pl.BlockSpec(memory_space=pltpu.VMEM)
SMEM = pl.BlockSpec(memory_space=pltpu.SMEM)
NT = (((1,), (1,)), ((), ()))


def three(v):
    high = v.astype(BF16).astype(F32)
    rest = v - high
    mid = rest.astype(BF16).astype(F32)
    return high, mid, rest - mid


def features(geo):
    high, mid, low = three(geo[0:3])
    norm = (
        geo[0:1] * geo[0:1] + geo[1:2] * geo[1:2] + geo[2:3] * geo[2:3] + geo[3:4] * geo[3:4]
    )
    nh, nm, nl = three(norm)
    one = jnp.ones_like(norm)
    pad = jnp.zeros((7, geo.shape[1]), F32)
    left = [high, high, high, mid, mid, mid, low, low, low, nh, nm, nl, one, one, one, pad]
    h2, m2, l2 = -2.0 * high, -2.0 * mid, -2.0 * low
    right = [h2, m2, l2, h2, m2, l2, h2, m2, l2, one, one, one, nh, nm, nl, pad]
    return left, right


def shifted(row, col, steps):
    flat = lax.rem(row * COLS + col + (steps + 2 * ROWS * COLS), ROWS * COLS)
    return flat // COLS, lax.rem(flat, COLS)


def potential_kernel(
    geo_ref, chg_ref, ni_ref, nc_ref, nw_ref, cond_ref, pot_ref, tot_ref,
    feat, right, wown, woth, back, acc_u, acc_v, tile_a, tile_b,
    ug, uc, vg, vc, ac, xg, xc, sb, rb, su, sv, ru, rv,
    send_u, recv_u, send_v, recv_v, send_a, recv_a, send_x, recv_x, send_b, recv_b, send_r, recv_r,
):
    row = lax.axis_index("row")
    col = lax.axis_index("col")
    place = lax.rem(row, 8)
    base = row - place
    up1 = shifted(row, col, 1)
    down1 = shifted(row, col, -1)
    up257 = shifted(row, col, 257)
    down257 = shifted(row, col, -257)
    sends_v = lax.rem(up257[0], 8) != 0
    takes_v = place != 0

    def mate(step):
        return base + lax.rem(place + step, 8), col

    barrier = pltpu.get_barrier_semaphore()
    for other in (up1, down1, up257, down257):
        pl.semaphore_signal(barrier, inc=1, device_id=other, device_id_type=MESH)
    for step in range(1, 8):
        pl.semaphore_signal(barrier, inc=1, device_id=mate(step), device_id_type=MESH)

    def remote(src, dst, ssem, rsem, where):
        return pltpu.make_async_remote_copy(
            src_ref=src, dst_ref=dst, send_sem=ssem, recv_sem=rsem, device_id=where,
            device_id_type=MESH,
        )

    copies_u = [
        remote(geo_ref, ug, send_u.at[0], recv_u.at[0], up1),
        remote(chg_ref, uc, send_u.at[1], recv_u.at[1], up1),
    ]
    copies_v = [
        remote(geo_ref, vg, send_v.at[0], recv_v.at[0], up257),
        remote(chg_ref, vc, send_v.at[1], recv_v.at[1], up257),
    ]
    copy_a = remote(chg_ref, ac, send_a, recv_a, down1)

    def group_copies(step, geo, chg):
        return [
            remote(geo, xg.at[step], send_x.at[0, step], recv_x.at[0, step], mate(step)),
            remote(chg, xc.at[step], send_x.at[1, step], recv_x.at[1, step], mate(step)),
        ]

    def back_copy(step):
        return remote(sb.at[step], rb.at[step], send_b.at[step], recv_b.at[step], mate(8 - step))

    copy_ru = remote(su, ru, send_r.at[0], recv_r.at[0], down1)
    copy_rv = remote(sv, rv, send_r.at[1], recv_r.at[1], down257)

    own = geo_ref[...]
    feat[...] = jnp.concatenate(features(own)[0], axis=0).T.astype(BF16)
    wown[...] = (chg_ref[...].astype(F32) * (own[3:4] * own[3:4])).astype(BF16)
    pot_ref[...] = jnp.zeros_like(pot_ref)

    def visit(geo, chg):
        right[...] = jnp.concatenate(features(geo)[1], axis=0).astype(BF16)
        woth[...] = (chg.astype(F32) * (geo[3:4] * geo[3:4])).astype(BF16)
        back[...] = jnp.zeros_like(back)
        tiles = (tile_a, tile_b)

        def fill(r):
            squared = jnp.dot(
                feat[r * ROWBLK : (r + 1) * ROWBLK, :], right[...], preferred_element_type=F32
            )
            tiles[r % 2][...] = lax.rsqrt(squared).astype(BF16)

        fill(0)
        for r in range(BLOCK // ROWBLK):
            if r + 1 < BLOCK // ROWBLK:
                fill(r + 1)
            rows = slice(r * ROWBLK, (r + 1) * ROWBLK)
            tile = tiles[r % 2][...]
            pot_ref[:, rows] += lax.dot_general(woth[...], tile, NT, preferred_element_type=F32)
            back[...] += jnp.dot(wown[:, rows], tile, preferred_element_type=F32)

    visit(own, chg_ref[...])

    pl.semaphore_wait(barrier, 11)

    @pl.when(sends_v)
    def _():
        for copy in copies_v:
            copy.start()

    for copy in copies_u:
        copy.start()
    copy_a.start()

    for copy in copies_u:
        copy.wait_recv()
    for step in range(1, 8):

        @pl.when(place + step < 8)
        def _():
            for copy in group_copies(step, ug, uc):
                copy.start()

    visit(ug[...], uc[...])
    acc_u[...] = back[...]
    acc_v[...] = jnp.zeros_like(acc_v)

    copy_a.wait_recv()

    def near(g, carry):
        index = ni_ref[pl.ds(g, 1), :]
        lane = lax.broadcasted_iota(jnp.int32, (1, 128), 1)
        index = jnp.where(lane < nc_ref[g], index, -1)
        slot = lax.broadcasted_iota(jnp.int32, (BLOCK, 128), 0)
        taken = jnp.zeros((RHS, 128), F32)
        for part, ref in enumerate((uc, chg_ref, ac)):
            pick = jnp.where(slot == index - part * BLOCK, 1.0, 0.0).astype(BF16)
            taken = taken + jnp.dot(ref[...], pick, preferred_element_type=F32)
        columns = pl.ds(pl.multiple_of(g * 128, 128), 128)
        pot_ref[:, columns] += lax.dot_general(
            taken.astype(BF16), nw_ref[g], NT, preferred_element_type=F32
        )
        return carry

    lax.fori_loop(0, GROUPS, near, 0)

    def round_(step, carry):
        @pl.when((step == jnp.minimum(place + 1, 4)) & takes_v)
        def _():
            for copy in copies_v:
                copy.wait_recv()
            for other in range(1, 8):

                @pl.when(place + other >= 8)
                def _():
                    for copy in group_copies(other, vg, vc):
                        copy.start()

        for copy in group_copies(step, ug, uc):
            copy.wait_recv()
        visit(xg[step], xc[step])
        sb[step] = back[...].astype(BF16)
        back_copy(step).start()
        return carry

    lax.fori_loop(1, 8, round_, 0)

    def collect(step, carry):
        back_copy(step).wait_recv()
        got = rb[step].astype(F32)

        @pl.when(place + step < 8)
        def _():
            acc_u[...] += got

        @pl.when(place + step >= 8)
        def _():
            acc_v[...] += got

        return carry

    lax.fori_loop(1, 8, collect, 0)
    sv[...] = acc_v[...].astype(BF16)
    su[...] = acc_u[...].astype(BF16)

    @pl.when(takes_v)
    def _():
        copy_rv.start()

    copy_ru.start()
    copy_ru.wait_recv()
    pot_ref[...] += ru[...].astype(F32)

    @pl.when(sends_v)
    def _():
        copy_rv.wait_recv()
        pot_ref[...] += rv[...].astype(F32)

    scaled = pot_ref[...] * (own[3:4] * own[3:4])
    pieces = three(scaled)
    slot = lax.broadcasted_iota(jnp.int32, (128, BLOCK), 0)
    total = jnp.zeros((8, 128), F32)
    for quarter in range(4):
        member = jnp.where(slot == cond_ref[...] + RHS * quarter, 1.0, 0.0).astype(BF16)
        for piece in pieces:
            part = piece[quarter * 8 : quarter * 8 + 8].astype(BF16)
            total = total + lax.dot_general(part, member, NT, preferred_element_type=F32)
    tot_ref[...] = total

    for copy in copies_u:
        copy.wait_send()
    copy_a.wait_send()

    @pl.when(sends_v)
    def _():
        for copy in copies_v:
            copy.wait_send()

    @pl.when(takes_v)
    def _():
        copy_rv.wait_send()

    copy_ru.wait_send()

    def drain(step, carry):
        for copy in group_copies(step, ug, uc):
            copy.wait_send()
        back_copy(step).wait_send()
        return carry

    lax.fori_loop(1, 8, drain, 0)


def totals_kernel(local_ref, out_ref, s1, s2, s3, send, recv1, recv2, recv3):
    row = lax.axis_index("row")
    col = lax.axis_index("col")
    place = lax.rem(row, 8)
    zhigh = row // 8
    yplace = col // 8
    zlow = lax.rem(col, 8)
    zplace = zhigh * 8 + zlow

    def in_group(step):
        return zhigh * 8 + lax.rem(place + step, 8), col

    def in_y(step):
        return row, lax.rem(yplace + step, 4) * 8 + zlow

    def in_z(step):
        other = lax.rem(zplace + step, 16)
        return (other // 8) * 8 + place, yplace * 8 + lax.rem(other, 8)

    stages = (
        (8, place, in_group, s1, recv1),
        (4, yplace, in_y, s2, recv2),
        (16, zplace, in_z, s3, recv3),
    )
    barrier = pltpu.get_barrier_semaphore()
    for count, _, where, _, _ in stages:
        for step in range(1, count):
            pl.semaphore_signal(barrier, inc=1, device_id=where(step), device_id_type=MESH)
    pl.semaphore_wait(barrier, 25)

    value = local_ref[...]
    sent = 0
    copies = []
    for count, mine, where, slots, recv in stages:
        slots[mine] = value
        stage = []
        for step in range(1, count):
            stage.append(
                pltpu.make_async_remote_copy(
                    src_ref=slots.at[mine], dst_ref=slots.at[mine], send_sem=send.at[sent],
                    recv_sem=recv.at[step], device_id=where(step), device_id_type=MESH,
                )
            )
            sent += 1
        for copy in stage:
            copy.start()
        for copy in stage:
            copy.wait_recv()
        value = slots[0]
        for other in range(1, count):
            value = value + slots[other]
        copies += stage
    out_ref[...] = value
    for copy in copies:
        copy.wait_send()


def on_device(geometry, charges, near_index, near_count, near_weight, conductor):
    def slots(*shape):
        return pltpu.VMEM(shape, BF16)

    dma = pltpu.SemaphoreType.DMA
    potential, local = pl.pallas_call(
        potential_kernel,
        out_shape=(
            jax.ShapeDtypeStruct((RHS, BLOCK), F32),
            jax.ShapeDtypeStruct((8, 128), F32),
        ),
        in_specs=[VMEM, VMEM, VMEM, SMEM, VMEM, VMEM],
        out_specs=(VMEM, VMEM),
        scratch_shapes=[
            slots(BLOCK, 40), slots(40, BLOCK), slots(RHS, BLOCK), slots(RHS, BLOCK),
            pltpu.VMEM((RHS, BLOCK), F32), pltpu.VMEM((RHS, BLOCK), F32),
            pltpu.VMEM((RHS, BLOCK), F32), slots(ROWBLK, BLOCK), slots(ROWBLK, BLOCK),
            pltpu.VMEM((4, BLOCK), F32), slots(RHS, BLOCK), pltpu.VMEM((4, BLOCK), F32),
            slots(RHS, BLOCK), slots(RHS, BLOCK), pltpu.VMEM((8, 4, BLOCK), F32),
            slots(8, RHS, BLOCK), slots(8, RHS, BLOCK), slots(8, RHS, BLOCK),
            slots(RHS, BLOCK), slots(RHS, BLOCK), slots(RHS, BLOCK), slots(RHS, BLOCK),
            dma((2,)), dma((2,)), dma((2,)), dma((2,)), dma, dma, dma((2, 8)), dma((2, 8)),
            dma((8,)), dma((8,)), dma((2,)), dma((2,)),
        ],
        compiler_params=pltpu.CompilerParams(
            collective_id=0, has_side_effects=True, vmem_limit_bytes=48 * 2**20
        ),
        name="potential",
    )(geometry, charges, near_index, near_count, near_weight, conductor.reshape(1, BLOCK))
    packed = pl.pallas_call(
        totals_kernel,
        out_shape=jax.ShapeDtypeStruct((8, 128), F32),
        in_specs=[VMEM],
        out_specs=VMEM,
        scratch_shapes=[
            pltpu.VMEM((8, 8, 128), F32), pltpu.VMEM((4, 8, 128), F32),
            pltpu.VMEM((16, 8, 128), F32), dma((25,)), dma((8,)), dma((4,)), dma((16,)),
        ],
        compiler_params=pltpu.CompilerParams(collective_id=1, has_side_effects=True),
        name="totals",
    )(local)
    totals = packed.reshape(8, 4, RHS).transpose(1, 0, 2).reshape(RHS, RHS)
    return potential, totals


def solution(mesh):
    in_specs = (
        P(None, ("row", "col")),
        P(None, ("row", "col")),
        P(("row", "col"), None),
        P(("row", "col")),
        P(("row", "col"), None, None),
        P(("row", "col")),
    )
    out_specs = (P(None, ("row", "col")), P())
    return jax.shard_map(
        on_device, mesh=mesh, in_specs=in_specs, out_specs=out_specs, check_vma=False
    )
```

time: 449 us -> 135 us (0.30); the launches traced: 440 us -> 135 us
  starting transfers between devices: 209 us -> 0 us
  Pallas kernels: 0 us -> 128 us
  blocking collectives: 113 us -> 0 us
  matrix products: 87.9 us -> 0 us
  waiting for transfers between devices: 15.6 us -> 0 us
  other arithmetic: 8.44 us -> 0 us
    ppermute x26 -> x0, starting transfers between devices: 209 us -> none  [the longest x24 190 us: passed_along(): return lax.ppermute(value, axis, pairs)]
    pallas_call x0 -> x2, Pallas kernels: none -> 128 us  [the longest x1 99 us: on_device(): pl.pallas_call(potential_kernel, out_shape=(jax.ShapeDtypeStruct((RHS, BL...]
    psum x1 -> x0, blocking collectives: 113 us -> none  [on_device(): totals = lax.psum(local_totals, ('row', 'col'))]
    dot_general x104 -> x0, matrix products: 87.9 us -> none  [the longest x48 43.2 us: pair_products(): jnp.dot(own_w[:, start:start + rowblk], tile, preferred_element_type=jnp....]
    ppermute x26 -> x0, waiting for transfers between devices: 15.6 us -> none  [the longest x24 15.6 us: passed_along(): return lax.ppermute(value, axis, pairs)]
  transfers between devices with their start and end apart: 26 -> 0, of which waited for: 2 -> 0; matrix products, arithmetic and copies ran while one was open for 22% -> 0% of each run, Pallas kernels for 0% -> 0%
where the time goes in v1:
time: 135 us
  Pallas kernels  128 us (95%)
  local copies, waits for them, and re-layouts  5.98 us (4%)
    pallas_call x1, Pallas kernels, on_device(): pl.pallas_call(potential_kernel, out_shape=(jax.ShapeDtypeStruct((RHS, BL...  99 us
    pallas_call x1, Pallas kernels, on_device(): pl.pallas_call(totals_kernel, out_shape=jax.ShapeDtypeStruct((8, 128), F3...  29.4 us
    unnamed x13, local copies, waits for them, and re-layouts  3.89 us

profile of v1, /device:TPU:1, one launch (start us, length us, event | category | flops | bytes accessed | tf_op | source)
XLA Modules:
  0.0 135.0 jit_solution(12076458930328615256)
XLA Ops:
  0.6 0.0 copy-start.5
  0.6 0.0 copy-start.3
  0.7 0.7 reshape.13.cond_ref
  1.4 0.0 copy-done.5
  1.4 0.0 copy-done.3
  1.4 0.0 copy-start
  1.4 1.0 copy-done
  2.4 0.0 copy-start.1
  2.4 0.9 copy-done.1
  3.3 0.0 copy-start.2
  3.3 0.7 copy-done.2
  4.0 99.0 %potential.1 = (f32[32,1536]{1,0:T(8,128)S(1)}, f32[8,128]{1,0:T(8,128)S(1)}) custom-call(f32[4,1536]{1,0:T(4,128)S(1)} %copy-done.2, bf16[32,1536]{1,0:T(8,128)(2,1)S(1)} %copy-done.1, s32[12,128]{1,0:T(8,128)S(1)} %copy-done.3, s32[12]{0:T(128)S(1)} %copy-done.5, bf16[12,128,128]{2,1,0:T(8,128)(2,1)S(1)} %copy-done, s32[1,1536]{1,0:T(1,128)S(1)} %reshape.13.cond_ref), custom_call_target="tpu_custom_call" | custom-call | tf_op jit(solution)/shard_map/potential/pallas_call | solution.py:324
  103.0 0.0 copy-start.4
  103.0 0.6 copy-done.4
  103.6 29.4 %totals.1 = f32[8,128]{1,0:T(8,128)} custom-call(f32[8,128]{1,0:T(8,128)} %copy-done.4), custom_call_target="tpu_custom_call" | custom-call | tf_op jit(solution)/shard_map/totals/pallas_call | solution.py:348
  133.0 0.8 reshape.14
  133.7 0.6 copy.10
  134.3 0.7 copy.12
Async XLA Ops:
  0.6 0.7 copy-start.5
  0.6 0.7 copy-start.3
  1.4 1.0 copy-start
  2.4 0.9 copy-start.1
  3.3 0.7 copy-start.2
  103.0 0.6 copy-start.4

commit v2 on v1

v2 whole, which is shorter than its diff:
```python
import jax
import jax.numpy as jnp
from jax import lax
from jax.experimental import pallas as pl
from jax.experimental.pallas import tpu as pltpu
from jax.sharding import PartitionSpec as P

MESH = pl.DeviceIdType.MESH
BLOCK = 1536
HALVES = 2
HALF = BLOCK // HALVES
RHS = 32
GROUPS = 12
ROWBLK = 256
ROWS = 16
COLS = 32
SEND_FIRST = 4
SEND_SECOND = 7
F32 = jnp.float32
BF16 = jnp.bfloat16
VMEM = pl.BlockSpec(memory_space=pltpu.VMEM)
SMEM = pl.BlockSpec(memory_space=pltpu.SMEM)
HBM = pl.BlockSpec(memory_space=pltpu.HBM)
NT = (((1,), (1,)), ((), ()))


def three(v):
    high = v.astype(BF16).astype(F32)
    rest = v - high
    mid = rest.astype(BF16).astype(F32)
    return high, mid, rest - mid


def features(geo):
    high, mid, low = three(geo[0:3])
    norm = (
        geo[0:1] * geo[0:1] + geo[1:2] * geo[1:2] + geo[2:3] * geo[2:3] + geo[3:4] * geo[3:4]
    )
    nh, nm, nl = three(norm)
    one = jnp.ones_like(norm)
    pad = jnp.zeros((7, geo.shape[1]), F32)
    left = [high, high, high, mid, mid, mid, low, low, low, nh, nm, nl, one, one, one, pad]
    h2, m2, l2 = -2.0 * high, -2.0 * mid, -2.0 * low
    right = [h2, m2, l2, h2, m2, l2, h2, m2, l2, one, one, one, nh, nm, nl, pad]
    return left, right


def shifted(row, col, steps):
    flat = lax.rem(row * COLS + col + (steps + 2 * ROWS * COLS), ROWS * COLS)
    return flat // COLS, lax.rem(flat, COLS)


def member_totals(value, size, conductor):
    pieces = three(value * (size * size))
    slot = lax.broadcasted_iota(jnp.int32, (RHS, value.shape[1]), 0)
    member = jnp.where(slot == conductor, 1.0, 0.0).astype(BF16)
    total = jnp.zeros((RHS, RHS), F32)
    for piece in pieces:
        total = total + lax.dot_general(
            piece.astype(BF16), member, NT, preferred_element_type=F32
        )
    return total


def kernel(
    geo_in, chg_in, ni_in, nc_ref, nw_in, cond_in, pot_ref, tot_ref,
    geo, chg, ni, nw, cond, in_sem,
    feat, right, wown, woth, back, acc_w, keep, total, tile_a, tile_b,
    xg, xc, xk, ac, sp, sq, pb, rb, sy, ry, sh, rh, s1, s2, s3,
    send_w, recv_w, send_y, recv_y, send_a, recv_a, send_x, recv_x, send_p, recv_p,
    send_b, recv_b, send_m, recv_m, send_h, recv_h, send_t, recv1, recv2, recv3,
):
    row = lax.axis_index("row")
    col = lax.axis_index("col")
    zhigh = row // 8
    place = lax.rem(row, 8)
    chip = place // 2
    core = lax.rem(place, 2)
    yplace = col // 8
    zlow = lax.rem(col, 8)
    zplace = zhigh * 8 + zlow
    up1 = shifted(row, col, 1)
    down1 = shifted(row, col, -1)
    near_dst = shifted(row, col, jnp.where(zlow == 7, 257, 1))
    near_src = shifted(row, col, jnp.where(zlow == 0, -257, -1))
    mate = (lax.rem(row + 8, ROWS), col)
    partner = (zhigh * 8 + chip * 2 + 1 - core, col)
    near_up = zlow != 0
    near_flag = near_up.astype(jnp.int32)
    far = jnp.logical_not(near_up & (place == 0))
    upper_slot = 8 - near_flag
    early = jnp.where(near_up, place + 1, 7 - place)
    late = 8 - early
    lead = jnp.where(near_up, core, 1 - core)
    near_field_early = near_up & (zlow != 7)

    def peer(step):
        return zhigh * 8 + lax.rem(chip + step, 4) * 2 + core, col

    def in_group(step):
        return zhigh * 8 + lax.rem(place + step, 8), col

    def in_y(step):
        return row, lax.rem(yplace + step, 4) * 8 + zlow

    def in_z(step):
        other = lax.rem(zplace + step, 16)
        return (other // 8) * 8 + place, yplace * 8 + lax.rem(other, 8)

    barrier = pltpu.get_barrier_semaphore()
    for other in (mate, near_dst, near_src, up1, down1):
        pl.semaphore_signal(barrier, inc=1, device_id=other, device_id_type=MESH)
    for count, where in ((16, in_z), (4, in_y), (8, in_group)):
        for step in range(1, count):
            pl.semaphore_signal(barrier, inc=1, device_id=where(step), device_id_type=MESH)

    loads = [
        pltpu.make_async_copy(src, dst, in_sem.at[i])
        for i, (src, dst) in enumerate(
            ((geo_in, geo), (chg_in, chg), (ni_in, ni), (nw_in, nw), (cond_in, cond))
        )
    ]
    for load in loads:
        load.start()

    def remote(src, dst, ssem, rsem, where):
        return pltpu.make_async_remote_copy(
            src_ref=src, dst_ref=dst, send_sem=ssem, recv_sem=rsem, device_id=where,
            device_id_type=MESH,
        )

    def w_copies(half):
        lanes = pl.ds(half * HALF, HALF)
        return [
            remote(
                src.at[:, lanes], dst.at[half], send_w.at[i, half], recv_w.at[i, half], near_dst
            )
            for i, (src, dst) in enumerate(
                zip((geo, chg, cond), (xg.at[7], xc.at[7], xk.at[0]))
            )
        ]

    def y_copies(half):
        return [
            remote(
                ref.at[src, half], ref.at[dst, half], send_y.at[i, half], recv_y.at[i, half], mate
            )
            for i, (ref, src, dst) in enumerate(((xg, 7, 8), (xc, 7, 8), (xk, 0, 1)))
        ]

    copy_a = remote(chg, ac, send_a, recv_a, down1)

    def slot_copies(src, slot, half, where):
        return [
            remote(
                ref.at[src, half], ref.at[slot, half], send_x.at[i, slot, half],
                recv_x.at[i, slot, half], where,
            )
            for i, ref in enumerate((xg, xc))
        ]

    def spread(src, half, upward):
        @pl.when(core == 1 - upward)
        def _():
            for copy in slot_copies(src, 0, half, partner):
                copy.start()

        for step in range(1, 4):

            @pl.when((chip + step < 4) == (upward == 1))
            def _():
                for copy in slot_copies(src, step, half, peer(step)):
                    copy.start()

    def partner_back(step, half):
        return remote(
            sp.at[step, half], pb.at[step, half], send_p.at[step, half], recv_p.at[step, half],
            partner,
        )

    def peer_back(step, half):
        return remote(
            sq.at[step, half], rb.at[step, half], send_b.at[step, half], recv_b.at[step, half],
            peer(4 - step),
        )

    def to_mate(half):
        return remote(sy.at[half], ry.at[half], send_m.at[half], recv_m.at[half], mate)

    def home(half):
        return remote(sh.at[half], rh.at[half], send_h.at[half], recv_h.at[half], near_src)

    for load in loads:
        load.wait()
    own = geo[...]
    feat[...] = jnp.concatenate(features(own)[0], axis=0).T.astype(BF16)
    wown[...] = (chg[...].astype(F32) * (own[3:4] * own[3:4])).astype(BF16)
    pot_ref[...] = jnp.zeros_like(pot_ref)

    def visit(other_geo, other_chg):
        right[...] = jnp.concatenate(features(other_geo)[1], axis=0).astype(BF16)
        woth[...] = (other_chg.astype(F32) * (other_geo[3:4] * other_geo[3:4])).astype(BF16)
        back[...] = jnp.zeros_like(back)
        tiles = (tile_a, tile_b)

        def fill(r):
            squared = jnp.dot(
                feat[r * ROWBLK : (r + 1) * ROWBLK, :], right[...], preferred_element_type=F32
            )
            tiles[r % 2][...] = lax.rsqrt(squared).astype(BF16)

        fill(0)
        for r in range(BLOCK // ROWBLK):
            if r + 1 < BLOCK // ROWBLK:
                fill(r + 1)
            rows = slice(r * ROWBLK, (r + 1) * ROWBLK)
            tile = tiles[r % 2][...]
            pot_ref[:, rows] += lax.dot_general(woth[...], tile, NT, preferred_element_type=F32)
            back[...] += jnp.dot(wown[:, rows], tile, preferred_element_type=F32)

    def own_half(half):
        lanes = pl.ds(pl.multiple_of(half * HALF, HALF), HALF)
        visit(geo[:, lanes], chg[:, lanes])

    own_half(0)
    pl.semaphore_wait(barrier, 30)
    for half in range(HALVES):
        for copy in w_copies(half):
            copy.start()
    copy_a.start()
    own_half(1)
    for half in range(HALVES):
        for copy in w_copies(half):
            copy.wait_recv()

        @pl.when(far)
        def _():
            for copy in y_copies(half):
                copy.start()

        spread(7, half, near_flag)

    def near_group(g, carry):
        index = ni[pl.ds(g, 1), :]
        lane = lax.broadcasted_iota(jnp.int32, (1, 128), 1)
        index = jnp.where(lane < nc_ref[g], index, -1)
        slot = lax.broadcasted_iota(jnp.int32, (HALF, 128), 0)
        taken = jnp.zeros((RHS, 128), F32)
        sources = (
            xc[upper_slot, 0], xc[upper_slot, 1], chg[:, :HALF], chg[:, HALF:],
            ac[:, :HALF], ac[:, HALF:],
        )
        for part, source in enumerate(sources):
            pick = jnp.where(slot == index - part * HALF, 1.0, 0.0).astype(BF16)
            taken = taken + jnp.dot(source, pick, preferred_element_type=F32)
        columns = pl.ds(pl.multiple_of(g * 128, 128), 128)
        pot_ref[:, columns] += lax.dot_general(
            taken.astype(BF16), nw[g], NT, preferred_element_type=F32
        )
        return carry

    def near_field():
        copy_a.wait_recv()
        lax.fori_loop(0, GROUPS, near_group, 0)

    pl.when(near_field_early)(near_field)

    def slot_of(t):
        rest = t - 2 * early
        is_late = rest >= 0
        second = rest >= late
        index = jnp.where(is_late, early + rest - jnp.where(second, late, 0), t // 2)
        half = jnp.where(is_late, second.astype(jnp.int32), lax.rem(t, 2))
        index = index - near_flag
        k = index - lead
        dist = jnp.where(near_up, k // 2 + 1, 3 - k // 2)
        slot = jnp.where((k < 0) | (k == 6), 0, dist + 3 * lax.rem(k + 2, 2))
        return jnp.where((index < 0) | (index == 7), upper_slot, slot), half

    def late_gather(t):
        slot, half = slot_of(jnp.maximum(t, 0))

        @pl.when((t >= 0) & (slot >= 1) & (slot <= 3))
        def _():
            partner_back(slot, half).wait_recv()
            sq[slot, half] = (keep[slot, half] + pb[slot, half].astype(F32)).astype(BF16)
            peer_back(slot, half).start()

    def step_(t, carry):
        for half, at in ((0, jnp.minimum(SEND_FIRST, 2 * early)),
                         (1, jnp.minimum(SEND_SECOND, 2 * early + late))):

            @pl.when((t == at) & far)
            def _():
                for copy in y_copies(half):
                    copy.wait_recv()
                spread(8, half, 1 - near_flag)

        slot, half = slot_of(t)
        direct = (slot >= 1) & (slot <= 3)

        @pl.when(slot < 7)
        def _():
            for copy in slot_copies(7, slot, half, partner):
                copy.wait_recv()

        @pl.when(direct)
        def _():
            for copy in slot_copies(slot, slot + 3, half, partner):
                copy.start()

        visit(xg[slot, half], xc[slot, half])

        @pl.when(direct)
        def _():
            keep[slot, half] = back[...]

        @pl.when(slot >= 7)
        def _():
            keep[0, half] = back[...]

        @pl.when((slot == 0) | ((slot >= 4) & (slot <= 6)))
        def _():
            step = jnp.where(slot == 0, 0, slot - 3)
            sp[step, half] = back[...].astype(BF16)
            partner_back(step, half).start()

        late_gather(t - 4)
        return carry

    lax.fori_loop(0, 16, step_, 0)

    def tail(t, carry):
        late_gather(t)
        return carry

    lax.fori_loop(12, 16, tail, 0)
    total[...] = jnp.zeros_like(total)

    def collect(dst, half, upward):
        dst[half] = keep[0, half] * upward.astype(F32)

        @pl.when(core == 1 - upward)
        def _():
            partner_back(0, half).wait_recv()
            dst[half] += pb[0, half].astype(F32)

        for step in range(1, 4):

            @pl.when((chip + step < 4) == (upward == 1))
            def _():
                peer_back(step, half).wait_recv()
                dst[half] += rb[step, half].astype(F32)

    @pl.when(far)
    def _():
        def one(half, carry):
            collect(acc_w, half, 1 - near_flag)
            sy[half] = acc_w[half].astype(BF16)
            to_mate(half).start()
            return carry

        lax.fori_loop(0, HALVES, one, 0)

        def more(half, carry):
            total[...] += member_totals(acc_w[half], xg[8, half][3:4], xk[1, half])
            return carry

        lax.fori_loop(0, HALVES, more, 0)

    def near_sum(half, carry):
        collect(acc_w, half, near_flag)
        total[...] += member_totals(acc_w[half], xg[7, half][3:4], xk[0, half])
        return carry

    lax.fori_loop(0, HALVES, near_sum, 0)
    pl.when(jnp.logical_not(near_field_early))(near_field)
    total[...] += member_totals(pot_ref[...], own[3:4], cond[...])

    local = total[...]
    value = jnp.concatenate([local[q * 8 : q * 8 + 8] for q in range(4)], axis=1)
    sent = 0
    total_copies = []
    for count, mine, where, slots, recv in (
        (8, place, in_group, s1, recv1),
        (4, yplace, in_y, s2, recv2),
        (16, zplace, in_z, s3, recv3),
    ):
        slots[mine] = value
        stage = []
        for step in range(1, count):
            stage.append(
                remote(slots.at[mine], slots.at[mine], send_t.at[sent], recv.at[step], where(step))
            )
            sent += 1
        for copy in stage:
            copy.start()
        if count == 16:
            for half in range(HALVES):

                @pl.when(far)
                def _():
                    to_mate(half).wait_recv()
                    acc_w[half] += ry[half].astype(F32)

                sh[half] = acc_w[half].astype(BF16)
                home(half).start()
        for copy in stage:
            copy.wait_recv()
        value = slots[0]
        for other in range(1, count):
            value = value + slots[other]
        total_copies += stage
    tot_ref[...] = value

    for half in range(HALVES):
        lanes = slice(half * HALF, (half + 1) * HALF)
        home(half).wait_recv()
        pot_ref[:, lanes] += rh[half].astype(F32)

    copy_a.wait_send()
    for copy in total_copies:
        copy.wait_send()

    def drain(half, carry):
        for copy in w_copies(half):
            copy.wait_send()
        home(half).wait_send()

        @pl.when(far)
        def _():
            for copy in y_copies(half):
                copy.wait_send()
            to_mate(half).wait_send()

        for slot in range(7):
            for copy in slot_copies(7, slot, half, partner):
                copy.wait_send()
        for step in range(4):
            partner_back(step, half).wait_send()
        for step in range(1, 4):
            peer_back(step, half).wait_send()
        return carry

    lax.fori_loop(0, HALVES, drain, 0)


def on_device(geometry, charges, near_index, near_count, near_weight, conductor):
    def half(kind, *lead, rows=RHS):
        return pltpu.VMEM((*lead, HALVES, rows, HALF), kind)

    dma = pltpu.SemaphoreType.DMA
    potential, packed = pl.pallas_call(
        kernel,
        out_shape=(
            jax.ShapeDtypeStruct((RHS, BLOCK), F32),
            jax.ShapeDtypeStruct((8, 128), F32),
        ),
        in_specs=[HBM, HBM, HBM, SMEM, HBM, HBM],
        out_specs=(VMEM, VMEM),
        scratch_shapes=[
            pltpu.VMEM((4, BLOCK), F32), pltpu.VMEM((RHS, BLOCK), BF16),
            pltpu.VMEM((GROUPS, 128), jnp.int32), pltpu.VMEM((GROUPS, 128, 128), BF16),
            pltpu.VMEM((1, BLOCK), jnp.int32), dma((5,)),
            pltpu.VMEM((BLOCK, 40), BF16), pltpu.VMEM((40, HALF), BF16),
            pltpu.VMEM((RHS, BLOCK), BF16), pltpu.VMEM((RHS, HALF), BF16),
            pltpu.VMEM((RHS, HALF), F32), half(F32), half(F32, 4), pltpu.VMEM((RHS, RHS), F32),
            pltpu.VMEM((ROWBLK, HALF), BF16), pltpu.VMEM((ROWBLK, HALF), BF16),
            half(F32, 9, rows=4), half(BF16, 9), half(jnp.int32, 2, rows=1),
            pltpu.VMEM((RHS, BLOCK), BF16), half(BF16, 4), half(BF16, 4), half(BF16, 4),
            half(BF16, 4), half(BF16), half(BF16), half(BF16), half(BF16),
            pltpu.VMEM((8, 8, 128), F32), pltpu.VMEM((4, 8, 128), F32),
            pltpu.VMEM((16, 8, 128), F32),
            dma((3, 2)), dma((3, 2)), dma((3, 2)), dma((3, 2)), dma, dma,
            dma((2, 7, 2)), dma((2, 7, 2)), dma((4, 2)), dma((4, 2)), dma((4, 2)), dma((4, 2)),
            dma((2,)), dma((2,)), dma((2,)), dma((2,)), dma((25,)), dma((8,)), dma((4,)),
            dma((16,)),
        ],
        compiler_params=pltpu.CompilerParams(
            collective_id=0, has_side_effects=True, vmem_limit_bytes=48 * 2**20
        ),
        name="potential",
    )(geometry, charges, near_index, near_count, near_weight, conductor.reshape(1, BLOCK))
    totals = packed.reshape(8, 4, RHS).transpose(1, 0, 2).reshape(RHS, RHS)
    return potential, totals


def solution(mesh):
    in_specs = (
        P(None, ("row", "col")),
        P(None, ("row", "col")),
        P(("row", "col"), None),
        P(("row", "col")),
        P(("row", "col"), None, None),
        P(("row", "col")),
    )
    out_specs = (P(None, ("row", "col")), P())
    return jax.shard_map(
        on_device, mesh=mesh, in_specs=in_specs, out_specs=out_specs, check_vma=False
    )
```

time: 135 us -> 95.6 us (0.71)
  Pallas kernels: 128 us -> 89.1 us
    pallas_call x2 -> x1, Pallas kernels: 128 us -> 89.1 us  [on_device(): pl.pallas_call(kernel, out_shape=(jax.ShapeDtypeStruct((RHS, BLOCK), F32)...]
    unnamed x13 -> x11, local copies, waits for them, and re-layouts: 3.89 us -> 3.3 us
where the time goes in v2:
time: 95.6 us; the launch traced here: 94.5 us
  Pallas kernels  89.1 us (93%)
  local copies, waits for them, and re-layouts  4.71 us (5%)
    pallas_call x1, Pallas kernels, on_device(): pl.pallas_call(kernel, out_shape=(jax.ShapeDtypeStruct((RHS, BLOCK), F32)...  89.1 us
    unnamed x11, local copies, waits for them, and re-layouts  3.3 us

profile of v2, /device:TPU:1, one launch (start us, length us, event | category | flops | bytes accessed | tf_op | source)
XLA Modules:
  0.0 94.5 jit_solution(10242358250631396595)
XLA Ops:
  0.6 0.0 copy-start.4
  0.6 0.0 copy-start.3
  0.7 0.7 reshape.13.cond_in
  1.4 0.0 copy-done.4
  1.4 0.0 copy-done.3
  1.4 0.0 copy-start
  1.4 1.0 %copy-done = bf16[12,128,128]{2,1,0:T(8,128)(2,1)S(1)} copy-done((bf16[12,128,128]{2,1,0:T(8,128)(2,1)S(1)}, bf16[12,128,128]{2,1,0:T(8,128)(2,1)}, u32[]{:S(2)}) %copy-start) | copy-done | bytes 393240
  2.4 0.0 copy-start.1
  2.4 0.9 copy-done.1
  3.3 0.0 copy-start.2
  3.3 0.7 copy-done.2
  4.0 89.1 %potential.1 = (f32[32,1536]{1,0:T(8,128)S(1)}, f32[8,128]{1,0:T(8,128)S(1)}) custom-call(f32[4,1536]{1,0:T(4,128)S(1)} %copy-done.2, bf16[32,1536]{1,0:T(8,128)(2,1)S(1)} %copy-done.1, s32[12,128]{1,0:T(8,128)S(1)} %copy-done.3, s32[12]{0:T(128)S(1)} %copy-done.4, bf16[12,128,128]{2,1,0:T(8,128)(2,1)S(1)} %copy-done, s32[1,1536]{1,0:T(1,128)S(1)} %reshape.13.cond_in), custom_call_target="tpu_custom_call" | custom-call | tf_op jit(solution)/shard_map/potential/pallas_call | solution.py:453
  93.1 0.1 reshape.14
  93.2 0.6 copy.10
  93.8 0.7 copy.12
Async XLA Ops:
  0.6 0.7 copy-start.4
  0.6 0.7 copy-start.3
  1.4 1.0 %copy-start = (bf16[12,128,128]{2,1,0:T(8,128)(2,1)S(1)}, bf16[12,128,128]{2,1,0:T(8,128)(2,1)}, u32[]{:S(2)}) copy-start(bf16[12,128,128]{2,1,0:T(8,128)(2,1)} %nw_in.1) | copy-start | bytes 1179652
  2.4 0.9 copy-start.1
  3.3 0.7 copy-start.2

commit v3 on v2

--- a/solution.py
+++ b/solution.py
@@ -7,15 +7,16 @@
 
 MESH = pl.DeviceIdType.MESH
 BLOCK = 1536
-HALVES = 2
-HALF = BLOCK // HALVES
+CHUNKS = 2
+WIDTH = BLOCK // CHUNKS
 RHS = 32
 GROUPS = 12
 ROWBLK = 256
 ROWS = 16
 COLS = 32
-SEND_FIRST = 4
-SEND_SECOND = 7
+STEPS = 8 * CHUNKS
+PASS_ON = (4, 7)
+VMEM_BYTES = 62 * 2**20
 F32 = jnp.float32
 BF16 = jnp.bfloat16
 VMEM = pl.BlockSpec(memory_space=pltpu.VMEM)
@@ -65,7 +66,7 @@
 def kernel(
     geo_in, chg_in, ni_in, nc_ref, nw_in, cond_in, pot_ref, tot_ref,
     geo, chg, ni, nw, cond, in_sem,
-    feat, right, wown, woth, back, acc_w, keep, total, tile_a, tile_b,
+    feat, right, wown, woth, back, acc_w, keep, total, tile_a, tile_b, flip_a, flip_b,
     xg, xc, xk, ac, sp, sq, pb, rb, sy, ry, sh, rh, s1, s2, s3,
     send_w, recv_w, send_y, recv_y, send_a, recv_a, send_x, recv_x, send_p, recv_p,
     send_b, recv_b, send_m, recv_m, send_h, recv_h, send_t, recv1, recv2, recv3,
@@ -130,7 +131,7 @@
         )
 
     def w_copies(half):
-        lanes = pl.ds(half * HALF, HALF)
+        lanes = pl.ds(half * WIDTH, WIDTH)
         return [
             remote(
                 src.at[:, lanes], dst.at[half], send_w.at[i, half], recv_w.at[i, half], near_dst
@@ -201,35 +202,37 @@
         right[...] = jnp.concatenate(features(other_geo)[1], axis=0).astype(BF16)
         woth[...] = (other_chg.astype(F32) * (other_geo[3:4] * other_geo[3:4])).astype(BF16)
         back[...] = jnp.zeros_like(back)
-        tiles = (tile_a, tile_b)
+        tiles, flips = (tile_a, tile_b), (flip_a, flip_b)
 
         def fill(r):
             squared = jnp.dot(
                 feat[r * ROWBLK : (r + 1) * ROWBLK, :], right[...], preferred_element_type=F32
             )
-            tiles[r % 2][...] = lax.rsqrt(squared).astype(BF16)
+            tile = lax.rsqrt(squared).astype(BF16)
+            tiles[r % 2][...] = tile
+            flips[r % 2][...] = tile.T
 
         fill(0)
         for r in range(BLOCK // ROWBLK):
             if r + 1 < BLOCK // ROWBLK:
                 fill(r + 1)
             rows = slice(r * ROWBLK, (r + 1) * ROWBLK)
-            tile = tiles[r % 2][...]
-            pot_ref[:, rows] += lax.dot_general(woth[...], tile, NT, preferred_element_type=F32)
-            back[...] += jnp.dot(wown[:, rows], tile, preferred_element_type=F32)
+            pot_ref[:, rows] += jnp.dot(woth[...], flips[r % 2][...], preferred_element_type=F32)
+            back[...] += jnp.dot(wown[:, rows], tiles[r % 2][...], preferred_element_type=F32)
 
     def own_half(half):
-        lanes = pl.ds(pl.multiple_of(half * HALF, HALF), HALF)
+        lanes = pl.ds(pl.multiple_of(half * WIDTH, WIDTH), WIDTH)
         visit(geo[:, lanes], chg[:, lanes])
 
     own_half(0)
     pl.semaphore_wait(barrier, 30)
-    for half in range(HALVES):
+    for half in range(CHUNKS):
         for copy in w_copies(half):
             copy.start()
     copy_a.start()
-    own_half(1)
-    for half in range(HALVES):
+    for half in range(CHUNKS):
+        if half + 1 < CHUNKS:
+            own_half(half + 1)
         for copy in w_copies(half):
             copy.wait_recv()
 
@@ -244,14 +247,13 @@
         index = ni[pl.ds(g, 1), :]
         lane = lax.broadcasted_iota(jnp.int32, (1, 128), 1)
         index = jnp.where(lane < nc_ref[g], index, -1)
-        slot = lax.broadcasted_iota(jnp.int32, (HALF, 128), 0)
+        slot = lax.broadcasted_iota(jnp.int32, (WIDTH, 128), 0)
         taken = jnp.zeros((RHS, 128), F32)
-        sources = (
-            xc[upper_slot, 0], xc[upper_slot, 1], chg[:, :HALF], chg[:, HALF:],
-            ac[:, :HALF], ac[:, HALF:],
-        )
+        sources = [xc[upper_slot, c] for c in range(CHUNKS)]
+        for ref in (chg, ac):
+            sources += [ref[:, c * WIDTH : (c + 1) * WIDTH] for c in range(CHUNKS)]
         for part, source in enumerate(sources):
-            pick = jnp.where(slot == index - part * HALF, 1.0, 0.0).astype(BF16)
+            pick = jnp.where(slot == index - part * WIDTH, 1.0, 0.0).astype(BF16)
             taken = taken + jnp.dot(source, pick, preferred_element_type=F32)
         columns = pl.ds(pl.multiple_of(g * 128, 128), 128)
         pot_ref[:, columns] += lax.dot_general(
@@ -266,29 +268,32 @@
     pl.when(near_field_early)(near_field)
 
     def slot_of(t):
-        rest = t - 2 * early
+        rest = t - CHUNKS * early
         is_late = rest >= 0
-        second = rest >= late
-        index = jnp.where(is_late, early + rest - jnp.where(second, late, 0), t // 2)
-        half = jnp.where(is_late, second.astype(jnp.int32), lax.rem(t, 2))
+        turn = sum((rest >= c * late).astype(jnp.int32) for c in range(1, CHUNKS))
+        index = jnp.where(is_late, early + rest - turn * late, t // CHUNKS)
+        half = jnp.where(is_late, turn, lax.rem(t, CHUNKS))
         index = index - near_flag
         k = index - lead
         dist = jnp.where(near_up, k // 2 + 1, 3 - k // 2)
         slot = jnp.where((k < 0) | (k == 6), 0, dist + 3 * lax.rem(k + 2, 2))
         return jnp.where((index < 0) | (index == 7), upper_slot, slot), half
 
-    def late_gather(t):
+    def gather(t, wanted):
         slot, half = slot_of(jnp.maximum(t, 0))
 
-        @pl.when((t >= 0) & (slot >= 1) & (slot <= 3))
+        @pl.when(wanted & (t >= 0) & (slot >= 1) & (slot <= 3))
         def _():
             partner_back(slot, half).wait_recv()
             sq[slot, half] = (keep[slot, half] + pb[slot, half].astype(F32)).astype(BF16)
             peer_back(slot, half).start()
 
+    def is_early(t):
+        return t < CHUNKS * early
+
     def step_(t, carry):
-        for half, at in ((0, jnp.minimum(SEND_FIRST, 2 * early)),
-                         (1, jnp.minimum(SEND_SECOND, 2 * early + late))):
+        for half in range(CHUNKS):
+            at = jnp.minimum(PASS_ON[half], CHUNKS * early + half * late)
 
             @pl.when((t == at) & far)
             def _():
@@ -325,16 +330,17 @@
             sp[step, half] = back[...].astype(BF16)
             partner_back(step, half).start()
 
-        late_gather(t - 4)
+        gather(t - 2 * CHUNKS, is_early(t - 2 * CHUNKS))
+        gather(t - 4, jnp.logical_not(is_early(t - 4)))
         return carry
 
-    lax.fori_loop(0, 16, step_, 0)
+    lax.fori_loop(0, STEPS, step_, 0)
 
     def tail(t, carry):
-        late_gather(t)
+        gather(t, is_early(t) | (t >= STEPS - 4))
         return carry
 
-    lax.fori_loop(12, 16, tail, 0)
+    lax.fori_loop(STEPS - 2 * CHUNKS, STEPS, tail, 0)
     total[...] = jnp.zeros_like(total)
 
     def collect(dst, half, upward):
@@ -360,20 +366,20 @@
             to_mate(half).start()
             return carry
 
-        lax.fori_loop(0, HALVES, one, 0)
+        lax.fori_loop(0, CHUNKS, one, 0)
 
         def more(half, carry):
             total[...] += member_totals(acc_w[half], xg[8, half][3:4], xk[1, half])
             return carry
 
-        lax.fori_loop(0, HALVES, more, 0)
+        lax.fori_loop(0, CHUNKS, more, 0)
 
     def near_sum(half, carry):
         collect(acc_w, half, near_flag)
         total[...] += member_totals(acc_w[half], xg[7, half][3:4], xk[0, half])
         return carry
 
-    lax.fori_loop(0, HALVES, near_sum, 0)
+    lax.fori_loop(0, CHUNKS, near_sum, 0)
     pl.when(jnp.logical_not(near_field_early))(near_field)
     total[...] += member_totals(pot_ref[...], own[3:4], cond[...])
 
@@ -396,7 +402,7 @@
         for copy in stage:
             copy.start()
         if count == 16:
-            for half in range(HALVES):
+            for half in range(CHUNKS):
 
                 @pl.when(far)
                 def _():
@@ -411,10 +417,11 @@
         for other in range(1, count):
             value = value + slots[other]
         total_copies += stage
-    tot_ref[...] = value
-
-    for half in range(HALVES):
-        lanes = slice(half * HALF, (half + 1) * HALF)
+    for q in range(4):
+        tot_ref[q * 8 : q * 8 + 8, :] = value[:, q * RHS : (q + 1) * RHS]
+
+    for half in range(CHUNKS):
+        lanes = slice(half * WIDTH, (half + 1) * WIDTH)
         home(half).wait_recv()
         pot_ref[:, lanes] += rh[half].astype(F32)
 
@@ -442,19 +449,19 @@
             peer_back(step, half).wait_send()
         return carry
 
-    lax.fori_loop(0, HALVES, drain, 0)
+    lax.fori_loop(0, CHUNKS, drain, 0)
 
 
 def on_device(geometry, charges, near_index, near_count, near_weight, conductor):
     def half(kind, *lead, rows=RHS):
-        return pltpu.VMEM((*lead, HALVES, rows, HALF), kind)
+        return pltpu.VMEM((*lead, CHUNKS, rows, WIDTH), kind)
 
     dma = pltpu.SemaphoreType.DMA
-    potential, packed = pl.pallas_call(
+    potential, totals = pl.pallas_call(
         kernel,
         out_shape=(
             jax.ShapeDtypeStruct((RHS, BLOCK), F32),
-            jax.ShapeDtypeStruct((8, 128), F32),
+            jax.ShapeDtypeStruct((RHS, RHS), F32),
         ),
         in_specs=[HBM, HBM, HBM, SMEM, HBM, HBM],
         out_specs=(VMEM, VMEM),
@@ -462,26 +469,24 @@
             pltpu.VMEM((4, BLOCK), F32), pltpu.VMEM((RHS, BLOCK), BF16),
             pltpu.VMEM((GROUPS, 128), jnp.int32), pltpu.VMEM((GROUPS, 128, 128), BF16),
             pltpu.VMEM((1, BLOCK), jnp.int32), dma((5,)),
-            pltpu.VMEM((BLOCK, 40), BF16), pltpu.VMEM((40, HALF), BF16),
-            pltpu.VMEM((RHS, BLOCK), BF16), pltpu.VMEM((RHS, HALF), BF16),
-            pltpu.VMEM((RHS, HALF), F32), half(F32), half(F32, 4), pltpu.VMEM((RHS, RHS), F32),
-            pltpu.VMEM((ROWBLK, HALF), BF16), pltpu.VMEM((ROWBLK, HALF), BF16),
+            pltpu.VMEM((BLOCK, 40), BF16), pltpu.VMEM((40, WIDTH), BF16),
+            pltpu.VMEM((RHS, BLOCK), BF16), pltpu.VMEM((RHS, WIDTH), BF16),
+            pltpu.VMEM((RHS, WIDTH), F32), half(F32), half(F32, 4), pltpu.VMEM((RHS, RHS), F32),
+            *[pltpu.VMEM((ROWBLK, WIDTH), BF16)] * 2, *[pltpu.VMEM((WIDTH, ROWBLK), BF16)] * 2,
             half(F32, 9, rows=4), half(BF16, 9), half(jnp.int32, 2, rows=1),
             pltpu.VMEM((RHS, BLOCK), BF16), half(BF16, 4), half(BF16, 4), half(BF16, 4),
             half(BF16, 4), half(BF16), half(BF16), half(BF16), half(BF16),
             pltpu.VMEM((8, 8, 128), F32), pltpu.VMEM((4, 8, 128), F32),
             pltpu.VMEM((16, 8, 128), F32),
-            dma((3, 2)), dma((3, 2)), dma((3, 2)), dma((3, 2)), dma, dma,
-            dma((2, 7, 2)), dma((2, 7, 2)), dma((4, 2)), dma((4, 2)), dma((4, 2)), dma((4, 2)),
-            dma((2,)), dma((2,)), dma((2,)), dma((2,)), dma((25,)), dma((8,)), dma((4,)),
+            *[dma((3, CHUNKS))] * 4, dma, dma, *[dma((2, 7, CHUNKS))] * 2,
+            *[dma((4, CHUNKS))] * 4, *[dma((CHUNKS,))] * 4, dma((25,)), dma((8,)), dma((4,)),
             dma((16,)),
         ],
         compiler_params=pltpu.CompilerParams(
-            collective_id=0, has_side_effects=True, vmem_limit_bytes=48 * 2**20
+            collective_id=0, has_side_effects=True, vmem_limit_bytes=VMEM_BYTES
         ),
         name="potential",
     )(geometry, charges, near_index, near_count, near_weight, conductor.reshape(1, BLOCK))
-    totals = packed.reshape(8, 4, RHS).transpose(1, 0, 2).reshape(RHS, RHS)
     return potential, totals
 
 

time: 95.6 us -> 93.6 us (0.979)
  local copies, waits for them, and re-layouts: 4.71 us -> 3.53 us
    unnamed x11 -> x4, local copies, waits for them, and re-layouts: 3.3 us -> 2.23 us
where the time goes in v3:
time: 93.6 us; the launch traced here: 93.2 us
  Pallas kernels  89 us (95%)
  local copies, waits for them, and re-layouts  3.53 us (4%)
    pallas_call x1, Pallas kernels, on_device(): pl.pallas_call(kernel, out_shape=(jax.ShapeDtypeStruct((RHS, BLOCK), F32)...  89 us
    unnamed x4, local copies, waits for them, and re-layouts  2.23 us

profile of v3, /device:TPU:1, one launch (start us, length us, event | category | flops | bytes accessed | tf_op | source)
XLA Modules:
  0.0 93.2 jit_solution(10619137526906594097)
XLA Ops:
  0.6 1.3 %reshape.7.cond_in = s32[1,1536]{1,0:T(1,128)} reshape(s32[1536]{0:T(1024)} %param.11) | data formatting | bytes 12288 | tf_op jit(solution)/shard_map/reshape | solution.py:489
  1.9 89.0 %potential.1 = (f32[32,1536]{1,0:T(8,128)}, f32[32,32]{1,0:T(8,128)}) custom-call(f32[4,1536]{1,0:T(4,128)} %geo_in.1, bf16[32,1536]{1,0:T(8,128)(2,1)} %chg_in.1, s32[12,128]{1,0:T(8,128)} %ni_in.1, s32[12]{0:T(128)} %nc_ref.1, bf16[12,128,128]{2,1,0:T(8,128)(2,1)} %nw_in.1, s32[1,1536]{1,0:T(1,128)} %reshape.7.cond_in), custom_call_target="tpu_custom_call" | custom-call | tf_op jit(solution)/shard_map/potential/pallas_call | solution.py:460
  91.0 0.0 copy-start
  91.0 1.6 %copy.10 = f32[32,1536]{1,0:T(8,128)} copy(f32[32,1536]{1,0:T(8,128)} %get-tuple-element.4) | data formatting | bytes 393216
  92.6 0.0 copy-done
  92.6 0.6 copy.11
Async XLA Ops:
  91.0 1.6 %copy-start = (f32[32,32]{1,0:T(8,128)S(1)}, f32[32,32]{1,0:T(8,128)}, u32[]{:S(2)}) copy-start(f32[32,32]{1,0:T(8,128)} %get-tuple-element.5) | copy-start | bytes 12292

commit v4 on v3

--- a/solution.py
+++ b/solution.py
@@ -11,11 +11,12 @@
 WIDTH = BLOCK // CHUNKS
 RHS = 32
 GROUPS = 12
-ROWBLK = 256
+ROWBLK = 384
 ROWS = 16
 COLS = 32
 STEPS = 8 * CHUNKS
 PASS_ON = (4, 7)
+FIRST_HOME = 4
 VMEM_BYTES = 62 * 2**20
 F32 = jnp.float32
 BF16 = jnp.bfloat16
@@ -291,6 +292,26 @@
     def is_early(t):
         return t < CHUNKS * early
 
+    def collect(dst, half, upward):
+        dst[half] = keep[0, half] * upward.astype(F32)
+
+        @pl.when(core == 1 - upward)
+        def _():
+            partner_back(0, half).wait_recv()
+            dst[half] += pb[0, half].astype(F32)
+
+        for step in range(1, 4):
+
+            @pl.when((chip + step < 4) == (upward == 1))
+            def _():
+                peer_back(step, half).wait_recv()
+                dst[half] += rb[step, half].astype(F32)
+
+    def far_sum(half):
+        collect(acc_w, half, 1 - near_flag)
+        sy[half] = acc_w[half].astype(BF16)
+        to_mate(half).start()
+
     def step_(t, carry):
         for half in range(CHUNKS):
             at = jnp.minimum(PASS_ON[half], CHUNKS * early + half * late)
@@ -330,6 +351,10 @@
             sp[step, half] = back[...].astype(BF16)
             partner_back(step, half).start()
 
+        @pl.when((t == jnp.minimum(CHUNKS * early + late + FIRST_HOME, STEPS - 1)) & far)
+        def _():
+            far_sum(0)
+
         gather(t - 2 * CHUNKS, is_early(t - 2 * CHUNKS))
         gather(t - 4, jnp.logical_not(is_early(t - 4)))
         return carry
@@ -343,30 +368,9 @@
     lax.fori_loop(STEPS - 2 * CHUNKS, STEPS, tail, 0)
     total[...] = jnp.zeros_like(total)
 
-    def collect(dst, half, upward):
-        dst[half] = keep[0, half] * upward.astype(F32)
-
-        @pl.when(core == 1 - upward)
-        def _():
-            partner_back(0, half).wait_recv()
-            dst[half] += pb[0, half].astype(F32)
-
-        for step in range(1, 4):
-
-            @pl.when((chip + step < 4) == (upward == 1))
-            def _():
-                peer_back(step, half).wait_recv()
-                dst[half] += rb[step, half].astype(F32)
-
     @pl.when(far)
     def _():
-        def one(half, carry):
-            collect(acc_w, half, 1 - near_flag)
-            sy[half] = acc_w[half].astype(BF16)
-            to_mate(half).start()
-            return carry
-
-        lax.fori_loop(0, CHUNKS, one, 0)
+        far_sum(1)
 
         def more(half, carry):
             total[...] += member_totals(acc_w[half], xg[8, half][3:4], xk[1, half])

time: 93.6 us -> 93 us (level)
  no operation moved by 1% of the time
where the time goes in v4:
time: 93 us; the launch traced here: 92.8 us
  Pallas kernels  88.6 us (95%)
  local copies, waits for them, and re-layouts  3.53 us (4%)
    pallas_call x1, Pallas kernels, on_device(): pl.pallas_call(kernel, out_shape=(jax.ShapeDtypeStruct((RHS, BLOCK), F32)...  88.6 us
    unnamed x4, local copies, waits for them, and re-layouts  2.23 us

profile of v4, /device:TPU:1, one launch (start us, length us, event | category | flops | bytes accessed | tf_op | source)
XLA Modules:
  0.0 92.8 jit_solution(10243553430008231821)
XLA Ops:
  0.6 1.3 %reshape.7.cond_in = s32[1,1536]{1,0:T(1,128)} reshape(s32[1536]{0:T(1024)} %param.11) | data formatting | bytes 12288 | tf_op jit(solution)/shard_map/reshape | solution.py:493
  1.9 88.6 %potential.1 = (f32[32,1536]{1,0:T(8,128)}, f32[32,32]{1,0:T(8,128)}) custom-call(f32[4,1536]{1,0:T(4,128)} %geo_in.1, bf16[32,1536]{1,0:T(8,128)(2,1)} %chg_in.1, s32[12,128]{1,0:T(8,128)} %ni_in.1, s32[12]{0:T(128)} %nc_ref.1, bf16[12,128,128]{2,1,0:T(8,128)(2,1)} %nw_in.1, s32[1,1536]{1,0:T(1,128)} %reshape.7.cond_in), custom_call_target="tpu_custom_call" | custom-call | tf_op jit(solution)/shard_map/potential/pallas_call | solution.py:464
  90.6 0.0 copy-start
  90.6 1.6 %copy.10 = f32[32,1536]{1,0:T(8,128)} copy(f32[32,1536]{1,0:T(8,128)} %get-tuple-element.4) | data formatting | bytes 393216
  92.2 0.0 copy-done
  92.2 0.6 copy.11
Async XLA Ops:
  90.6 1.6 %copy-start = (f32[32,32]{1,0:T(8,128)S(1)}, f32[32,32]{1,0:T(8,128)}, u32[]{:S(2)}) copy-start(f32[32,32]{1,0:T(8,128)} %get-tuple-element.5) | copy-start | bytes 12292

commit v5 on v4

--- a/solution.py
+++ b/solution.py
@@ -67,7 +67,7 @@
 def kernel(
     geo_in, chg_in, ni_in, nc_ref, nw_in, cond_in, pot_ref, tot_ref,
     geo, chg, ni, nw, cond, in_sem,
-    feat, right, wown, woth, back, acc_w, keep, total, tile_a, tile_b, flip_a, flip_b,
+    feat, right, wown, woth, back, acc_w, acc_y, keep, total, tile_a, tile_b, flip_a, flip_b,
     xg, xc, xk, ac, sp, sq, pb, rb, sy, ry, sh, rh, s1, s2, s3,
     send_w, recv_w, send_y, recv_y, send_a, recv_a, send_x, recv_x, send_p, recv_p,
     send_b, recv_b, send_m, recv_m, send_h, recv_h, send_t, recv1, recv2, recv3,
@@ -308,8 +308,8 @@
                 dst[half] += rb[step, half].astype(F32)
 
     def far_sum(half):
-        collect(acc_w, half, 1 - near_flag)
-        sy[half] = acc_w[half].astype(BF16)
+        collect(acc_y, half, 1 - near_flag)
+        sy[half] = acc_y[half].astype(BF16)
         to_mate(half).start()
 
     def step_(t, carry):
@@ -366,17 +366,8 @@
         return carry
 
     lax.fori_loop(STEPS - 2 * CHUNKS, STEPS, tail, 0)
-    total[...] = jnp.zeros_like(total)
-
-    @pl.when(far)
-    def _():
-        far_sum(1)
-
-        def more(half, carry):
-            total[...] += member_totals(acc_w[half], xg[8, half][3:4], xk[1, half])
-            return carry
-
-        lax.fori_loop(0, CHUNKS, more, 0)
+    pl.when(jnp.logical_not(near_field_early))(near_field)
+    total[...] = member_totals(pot_ref[...], own[3:4], cond[...])
 
     def near_sum(half, carry):
         collect(acc_w, half, near_flag)
@@ -384,8 +375,12 @@
         return carry
 
     lax.fori_loop(0, CHUNKS, near_sum, 0)
-    pl.when(jnp.logical_not(near_field_early))(near_field)
-    total[...] += member_totals(pot_ref[...], own[3:4], cond[...])
+
+    @pl.when(far)
+    def _():
+        total[...] += member_totals(acc_y[0], xg[8, 0][3:4], xk[1, 0])
+        far_sum(1)
+        total[...] += member_totals(acc_y[1], xg[8, 1][3:4], xk[1, 1])
 
     local = total[...]
     value = jnp.concatenate([local[q * 8 : q * 8 + 8] for q in range(4)], axis=1)
@@ -475,7 +470,7 @@
             pltpu.VMEM((1, BLOCK), jnp.int32), dma((5,)),
             pltpu.VMEM((BLOCK, 40), BF16), pltpu.VMEM((40, WIDTH), BF16),
             pltpu.VMEM((RHS, BLOCK), BF16), pltpu.VMEM((RHS, WIDTH), BF16),
-            pltpu.VMEM((RHS, WIDTH), F32), half(F32), half(F32, 4), pltpu.VMEM((RHS, RHS), F32),
+            pltpu.VMEM((RHS, WIDTH), F32), half(F32), half(F32), half(F32, 4), pltpu.VMEM((RHS, RHS), F32),
             *[pltpu.VMEM((ROWBLK, WIDTH), BF16)] * 2, *[pltpu.VMEM((WIDTH, ROWBLK), BF16)] * 2,
             half(F32, 9, rows=4), half(BF16, 9), half(jnp.int32, 2, rows=1),
             pltpu.VMEM((RHS, BLOCK), BF16), half(BF16, 4), half(BF16, 4), half(BF16, 4),

time: 93 us -> 92.1 us (level); the launches traced: 92.8 us -> 90.6 us
  Pallas kernels: 88.6 us -> 86.5 us
    pallas_call x1, Pallas kernels: 88.6 us -> 86.5 us  [on_device(): pl.pallas_call(kernel, out_shape=(jax.ShapeDtypeStruct((RHS, BLOCK), F32)...]
where the time goes in v5:
time: 92.1 us; the launch traced here: 90.6 us
  Pallas kernels  86.5 us (94%)
  local copies, waits for them, and re-layouts  3.53 us (4%)
    pallas_call x1, Pallas kernels, on_device(): pl.pallas_call(kernel, out_shape=(jax.ShapeDtypeStruct((RHS, BLOCK), F32)...  86.5 us
    unnamed x4, local copies, waits for them, and re-layouts  2.23 us

profile of v5, /device:TPU:1, one launch (start us, length us, event | category | flops | bytes accessed | tf_op | source)
XLA Modules:
  0.0 90.6 jit_solution(3125413894182796115)
XLA Ops:
  0.6 1.3 %reshape.7.cond_in = s32[1,1536]{1,0:T(1,128)} reshape(s32[1536]{0:T(1024)} %param.11) | data formatting | bytes 12288 | tf_op jit(solution)/shard_map/reshape | solution.py:488
  1.9 86.5 %potential.1 = (f32[32,1536]{1,0:T(8,128)}, f32[32,32]{1,0:T(8,128)}) custom-call(f32[4,1536]{1,0:T(4,128)} %geo_in.1, bf16[32,1536]{1,0:T(8,128)(2,1)} %chg_in.1, s32[12,128]{1,0:T(8,128)} %ni_in.1, s32[12]{0:T(128)} %nc_ref.1, bf16[12,128,128]{2,1,0:T(8,128)(2,1)} %nw_in.1, s32[1,1536]{1,0:T(1,128)} %reshape.7.cond_in), custom_call_target="tpu_custom_call" | custom-call | tf_op jit(solution)/shard_map/potential/pallas_call | solution.py:459
  88.4 0.0 copy-start
  88.4 1.6 %copy.10 = f32[32,1536]{1,0:T(8,128)} copy(f32[32,1536]{1,0:T(8,128)} %get-tuple-element.4) | data formatting | bytes 393216
  90.0 0.0 copy-done
  90.0 0.6 copy.11
Async XLA Ops:
  88.4 1.6 %copy-start = (f32[32,32]{1,0:T(8,128)S(1)}, f32[32,32]{1,0:T(8,128)}, u32[]{:S(2)}) copy-start(f32[32,32]{1,0:T(8,128)} %get-tuple-element.5) | copy-start | bytes 12292

commit v6 on v5

--- a/solution.py
+++ b/solution.py
@@ -356,13 +356,13 @@
             far_sum(0)
 
         gather(t - 2 * CHUNKS, is_early(t - 2 * CHUNKS))
-        gather(t - 4, jnp.logical_not(is_early(t - 4)))
+        gather(t - 3, jnp.logical_not(is_early(t - 3)))
         return carry
 
     lax.fori_loop(0, STEPS, step_, 0)
 
     def tail(t, carry):
-        gather(t, is_early(t) | (t >= STEPS - 4))
+        gather(t, is_early(t) | (t >= STEPS - 3))
         return carry
 
     lax.fori_loop(STEPS - 2 * CHUNKS, STEPS, tail, 0)

time: 92.1 us -> 91 us (0.988)
  no operation moved by 1% of the time
where the time goes in v6:
time: 91 us; the launch traced here: 90.4 us
  Pallas kernels  86.3 us (95%)
  local copies, waits for them, and re-layouts  3.53 us (4%)
    pallas_call x1, Pallas kernels, on_device(): pl.pallas_call(kernel, out_shape=(jax.ShapeDtypeStruct((RHS, BLOCK), F32)...  86.3 us
    unnamed x4, local copies, waits for them, and re-layouts  2.23 us

profile of v6, /device:TPU:1, one launch (start us, length us, event | category | flops | bytes accessed | tf_op | source)
XLA Modules:
  0.0 90.4 jit_solution(17816876287307267082)
XLA Ops:
  0.6 1.3 %reshape.7.cond_in = s32[1,1536]{1,0:T(1,128)} reshape(s32[1536]{0:T(1024)} %param.11) | data formatting | bytes 12288 | tf_op jit(solution)/shard_map/reshape | solution.py:488
  1.9 86.3 %potential.1 = (f32[32,1536]{1,0:T(8,128)}, f32[32,32]{1,0:T(8,128)}) custom-call(f32[4,1536]{1,0:T(4,128)} %geo_in.1, bf16[32,1536]{1,0:T(8,128)(2,1)} %chg_in.1, s32[12,128]{1,0:T(8,128)} %ni_in.1, s32[12]{0:T(128)} %nc_ref.1, bf16[12,128,128]{2,1,0:T(8,128)(2,1)} %nw_in.1, s32[1,1536]{1,0:T(1,128)} %reshape.7.cond_in), custom_call_target="tpu_custom_call" | custom-call | tf_op jit(solution)/shard_map/potential/pallas_call | solution.py:459
  88.2 0.0 copy-start
  88.2 1.6 %copy.10 = f32[32,1536]{1,0:T(8,128)} copy(f32[32,1536]{1,0:T(8,128)} %get-tuple-element.4) | data formatting | bytes 393216
  89.8 0.0 copy-done
  89.8 0.6 copy.11
Async XLA Ops:
  88.2 1.6 %copy-start = (f32[32,32]{1,0:T(8,128)S(1)}, f32[32,32]{1,0:T(8,128)}, u32[]{:S(2)}) copy-start(f32[32,32]{1,0:T(8,128)} %get-tuple-element.5) | copy-start | bytes 12292
